TPU v7x, 8 devices: a whole 2x2x1 slice. The times are simulated.
8 devices in a mesh: dp: 1 (over z), tx: 2 (over y), ty: 4 (over x, core).
Axes of the slice: x: 2, y: 2, z: 1, core: 2. Of those that a mesh axis runs over, the one named last changes fastest.
Arguments:
- x_in: bfloat16 [6, 729, 1152], P('dp', None, 'tx')
- ln1_gain: float32 [2, 1152], P(None, 'tx')
- ln1_bias: float32 [2, 1152], P(None, 'tx')
- w_q: bfloat16 [2, 1152, 16, 72], P(None, 'tx', 'ty')
- b_q: float32 [2, 16, 72], P(None, 'ty')
- w_k: bfloat16 [2, 1152, 16, 72], P(None, 'tx', 'ty')
- w_v: bfloat16 [2, 1152, 16, 72], P(None, 'tx', 'ty')
- b_v: float32 [2, 16, 72], P(None, 'ty')
- w_o: bfloat16 [2, 16, 72, 1152], P(None, 'ty', None, 'tx')
- b_o: float32 [2, 1152], P(None, 'tx')
- ln2_gain: float32 [2, 1152], P(None, 'tx')
- ln2_bias: float32 [2, 1152], P(None, 'tx')
- w_up: bfloat16 [2, 1152, 4304], P(None, 'tx', 'ty')
- b_up: float32 [2, 4304], P(None, 'ty')
- w_down: bfloat16 [2, 4304, 1152], P(None, 'ty', 'tx')
- b_down: float32 [2, 1152], P(None, 'tx')
Outputs:
- output: bfloat16 [6, 729, 1152], P('dp', None, 'tx')
All inputs are finite; a program needn't handle non-finite values.
Results may differ from a plain program's by a relative error of at most 0.019374.
Values are sent between devices in bfloat16 or wider.
A program may use at most 1 GiB of HBM per device.

v0:
```python
import jax
import jax.numpy as jnp
from jax import lax
from jax.sharding import PartitionSpec as P

EPS = 1e-6


def split_norm(x_f, gain, shift, width):
    moments = lax.psum(jnp.stack([jnp.sum(x_f, axis=-1), jnp.sum(x_f * x_f, axis=-1)]), "tx")
    mean = (moments[0] / width)[..., None]
    variance = (moments[1] / width)[..., None] - mean * mean
    return ((x_f - mean) * lax.rsqrt(variance + EPS) * gain + shift).astype(jnp.bfloat16)


def solution(mesh):
    tx_size = mesh.shape["tx"]
    act_spec = P("dp", None, "tx")
    vec_tx = P(None, "tx")
    proj_spec = P(None, "tx", "ty", None)
    head_vec = P(None, "ty", None)
    in_specs = (act_spec, vec_tx, vec_tx, proj_spec, head_vec, proj_spec, proj_spec, head_vec,
                P(None, "ty", None, "tx"), vec_tx, vec_tx, vec_tx,
                P(None, "tx", "ty"), P(None, "ty"), P(None, "ty", "tx"), vec_tx)

    def local_fn(x_in, ln1_gain, ln1_bias, w_q, b_q, w_k, w_v, b_v, w_o, b_o, ln2_gain, ln2_bias, w_up, b_up, w_down, b_down):
        width = x_in.shape[-1] * tx_size
        scale = w_q.shape[-1] ** -0.5
        residual = x_in
        for layer in range(w_q.shape[0]):
            x_f = residual.astype(jnp.float32)
            normed = split_norm(x_f, ln1_gain[layer], ln1_bias[layer], width)
            part_q = jnp.einsum("bnw,whd->bnhd", normed, w_q[layer], preferred_element_type=jnp.float32).astype(jnp.bfloat16)
            part_k = jnp.einsum("bnw,whd->bnhd", normed, w_k[layer], preferred_element_type=jnp.float32).astype(jnp.bfloat16)
            part_v = jnp.einsum("bnw,whd->bnhd", normed, w_v[layer], preferred_element_type=jnp.float32).astype(jnp.bfloat16)
            sum_q, k_proj, sum_v = lax.psum((part_q, part_k, part_v), "tx")
            q_proj = (sum_q.astype(jnp.float32) + b_q[layer]).astype(jnp.bfloat16)
            v_proj = (sum_v.astype(jnp.float32) + b_v[layer]).astype(jnp.bfloat16)
            scores = jnp.einsum("bqhd,bkhd->bhqk", q_proj, k_proj, preferred_element_type=jnp.float32) * scale
            attn_prob = jax.nn.softmax(scores, axis=-1).astype(jnp.bfloat16)
            attended = jnp.einsum("bhqk,bkhd->bqhd", attn_prob, v_proj, preferred_element_type=jnp.float32).astype(jnp.bfloat16)
            part_o = jnp.einsum("bqhd,hdw->bqw", attended, w_o[layer], preferred_element_type=jnp.float32).astype(jnp.bfloat16)
            x_mid = (x_f + lax.psum(part_o, "ty").astype(jnp.float32) + b_o[layer]).astype(jnp.bfloat16)
            mid_f = x_mid.astype(jnp.float32)
            normed2 = split_norm(mid_f, ln2_gain[layer], ln2_bias[layer], width)
            part_up = jnp.einsum("bnw,wf->bnf", normed2, w_up[layer], preferred_element_type=jnp.float32).astype(jnp.bfloat16)
            hidden = jax.nn.gelu(lax.psum(part_up, "tx").astype(jnp.float32) + b_up[layer], approximate=True).astype(jnp.bfloat16)
            part_down = jnp.einsum("bnf,fw->bnw", hidden, w_down[layer], preferred_element_type=jnp.float32).astype(jnp.bfloat16)
            residual = (mid_f + lax.psum(part_down, "ty").astype(jnp.float32) + b_down[layer]).astype(jnp.bfloat16)
        return residual

    return jax.shard_map(local_fn, mesh=mesh, in_specs=in_specs, out_specs=act_spec, check_vma=False)
```

profile of v0, /device:TPU:0, one launch (start us, length us, event | category | flops | bytes accessed | tf_op | source)
XLA Modules:
  0.0 1487.5 jit_solution(2831820862841711529)
XLA Ops:
  6.5 4.0 convert_reduce_fusion.3
  10.6 10.8 psum.112
  21.4 0.8 slice_reduce_fusion.6
  22.3 7.2 convolution_convert_fusion.6
  29.5 4.5 convolution_convert_fusion.5
  34.1 4.5 convolution_convert_fusion.7
  39.5 182.2 %all-reduce.25.cloned.1.call-done = (bf16[6,729,4,72]{1,3,2,0:T(8,128)(2,1)}, bf16[6,729,4,72]{1,3,2,0:T(8,128)(2,1)}, bf16[6,729,4,72]{1,3,2,0:T(8,128)(2,1)}) async-done(((bf16[6,729,4,72]{1,3,2,0:T(8,128)(2,1)}, bf16[6,729,4,72]{1,3,2,0:T(8,128)(2,1)}, bf16[6,729,4,72]{1,3,2,0:T(8,128)(2,1)}), (bf16[6,729,4,72]{1,3,2,0:T(8,128)(2,1)}, bf16[6,729,4,72]{1,3,2,0:T(8,128)(2,1)}, ...) | async-done | bytes 7558288 | tf_op jit(solution)/shard_map/psum | solution.py:36
  221.7 25.7 %fusion.153 = (f32[6,4,729]{2,1,0:T(4,128)S(1)}, f32[6,4,729,729]{2,3,1,0:T(8,128)}) fusion(bf16[6,729,4,72]{1,3,2,0:T(8,128)(2,1)} %get-tuple-element.30, bf16[6,729,4,72]{1,3,2,0:T(8,128)(2,1)} %get-tuple-element.31, f32[4,72]{1,0:T(4,128)S(1)} %get-tuple-element.39), kind=kOutput, calls=%fused_computation.198 | convolution fusion | flops 1878703616 | bytes 56128320 | tf_op jit(solution)/shard_map/sub | solution.py:40
  247.4 22.8 %bitcast_convert_fusion.1 = bf16[6,729,576]{1,2,0:T(8,128)(2,1)} fusion(f32[6,4,729,729]{2,3,1,0:T(8,128)} %get-tuple-element.41, f32[6,4,729]{2,1,0:T(4,128)S(1)} %get-tuple-element.40, bf16[6,729,4,72]{1,3,2,0:T(8,128)(2,1)} %get-tuple-element.32, f32[4,72]{1,0:T(4,128)S(1)} %get-tuple-element.37, bf16[2,4,72,576]{3,2,1,0:T(8,128)(2,1)S(1)} %copy-done.13), kind=kOutput, calls=%fused_computation.79 | convolution fusion | flops 3320915968 | bytes 59021024 | tf_op jit(solution)/shard_map/bqhd,hdw->bqw/dot_general | solution.py:42
  271.0 97.3 %all-reduce.11.cloned.1.call-done = bf16[6,729,576]{1,2,0:T(8,128)(2,1)} async-done(((bf16[6,729,576]{1,2,0:T(8,128)(2,1)}), bf16[6,729,576]{1,2,0:T(8,128)(2,1)}) %all-reduce.11.cloned.1.call-update) | async-done | bytes 5038864 | tf_op jit(solution)/shard_map/psum | solution.py:43
  368.3 8.6 convert_reduce_fusion.2
  376.8 9.2 psum.117
  386.1 13.3 convolution_convert_fusion.1
  399.5 225.1 %all-reduce.13.cloned.1.call-done = bf16[6,729,1076]{1,2,0:T(8,128)(2,1)} async-done(((bf16[6,729,1076]{1,2,0:T(8,128)(2,1)}), bf16[6,729,1076]{1,2,0:T(8,128)(2,1)}) %all-reduce.13.cloned.1.call-update) | async-done | bytes 9412864 | tf_op jit(solution)/shard_map/psum | solution.py:47
  624.6 15.5 %fusion.76 = bf16[6,729,576]{1,2,0:T(8,128)(2,1)} fusion(bf16[6,729,1076]{1,2,0:T(8,128)(2,1)} %all-reduce.13.cloned.1.call-done, f32[1076]{0:T(1024)S(1)} %get-tuple-element.14, bf16[2,1076,576]{1,2,0:T(8,128)(2,1)} %param.30), kind=kOutput, calls=%fused_computation.98 | convolution fusion | flops 5476090880 | bytes 16323536 | tf_op jit(solution)/shard_map/bnf,fw->bnw/dot_general | solution.py:48
  640.2 98.4 %all-reduce.15.cloned.1.call-done = bf16[6,729,576]{1,2,0:T(8,128)(2,1)} async-done(((bf16[6,729,576]{1,2,0:T(8,128)(2,1)}), bf16[6,729,576]{1,2,0:T(8,128)(2,1)}) %all-reduce.15.cloned.1.call-update) | async-done | bytes 5038864 | tf_op jit(solution)/shard_map/psum | solution.py:49
  738.7 8.6 convert_reduce_fusion.1
  747.2 9.1 psum.120
  756.4 7.2 convolution_convert_fusion.3
  763.6 4.5 convolution_convert_fusion.2
  768.1 4.5 convolution_convert_fusion.4
  772.9 182.0 %all-reduce.23.cloned.1.call-done = (bf16[6,729,4,72]{1,3,2,0:T(8,128)(2,1)}, bf16[6,729,4,72]{1,3,2,0:T(8,128)(2,1)}, bf16[6,729,4,72]{1,3,2,0:T(8,128)(2,1)}) async-done(((bf16[6,729,4,72]{1,3,2,0:T(8,128)(2,1)}, bf16[6,729,4,72]{1,3,2,0:T(8,128)(2,1)}, bf16[6,729,4,72]{1,3,2,0:T(8,128)(2,1)}), (bf16[6,729,4,72]{1,3,2,0:T(8,128)(2,1)}, bf16[6,729,4,72]{1,3,2,0:T(8,128)(2,1)}, ...) | async-done | bytes 7558288 | tf_op jit(solution)/shard_map/psum | solution.py:36
  954.9 25.7 %fusion.154 = (f32[6,4,729]{2,1,0:T(4,128)S(1)}, f32[6,4,729,729]{2,3,1,0:T(8,128)}) fusion(bf16[6,729,4,72]{1,3,2,0:T(8,128)(2,1)} %get-tuple-element.27, bf16[6,729,4,72]{1,3,2,0:T(8,128)(2,1)} %get-tuple-element.28, f32[4,72]{1,0:T(4,128)S(1)} %get-tuple-element.38), kind=kOutput, calls=%fused_computation.199 | convolution fusion | flops 1878703616 | bytes 56128320 | tf_op jit(solution)/shard_map/sub | solution.py:40
  980.6 22.9 %bitcast_convert_fusion = bf16[6,729,576]{1,2,0:T(8,128)(2,1)} fusion(f32[6,4,729,729]{2,3,1,0:T(8,128)} %get-tuple-element.43, f32[6,4,729]{2,1,0:T(4,128)S(1)} %get-tuple-element.42, bf16[6,729,4,72]{1,3,2,0:T(8,128)(2,1)} %get-tuple-element.29, f32[4,72]{1,0:T(4,128)S(1)} %copy-done.9, bf16[2,4,72,576]{3,2,1,0:T(8,128)(2,1)S(1)} %copy-done.14), kind=kOutput, calls=%fused_computation.78 | convolution fusion | flops 3320915968 | bytes 59021024 | tf_op jit(solution)/shard_map/bqhd,hdw->bqw/dot_general | solution.py:42
  1003.6 98.0 %all-reduce.17.cloned.1.call-done = bf16[6,729,576]{1,2,0:T(8,128)(2,1)} async-done(((bf16[6,729,576]{1,2,0:T(8,128)(2,1)}), bf16[6,729,576]{1,2,0:T(8,128)(2,1)}) %all-reduce.17.cloned.1.call-update) | async-done | bytes 5038864 | tf_op jit(solution)/shard_map/psum | solution.py:43
  1101.6 8.6 convert_reduce_fusion
  1110.1 9.0 psum.125
  1119.2 13.3 convolution_convert_fusion
  1132.6 225.1 %all-reduce.19.cloned.1.call-done = bf16[6,729,1076]{1,2,0:T(8,128)(2,1)} async-done(((bf16[6,729,1076]{1,2,0:T(8,128)(2,1)}), bf16[6,729,1076]{1,2,0:T(8,128)(2,1)}) %all-reduce.19.cloned.1.call-update) | async-done | bytes 9412864 | tf_op jit(solution)/shard_map/psum | solution.py:47
  1357.7 15.5 %fusion.79 = bf16[6,729,576]{1,2,0:T(8,128)(2,1)} fusion(bf16[6,729,1076]{1,2,0:T(8,128)(2,1)} %all-reduce.19.cloned.1.call-done, f32[1076]{0:T(1024)S(1)} %get-tuple-element.13, bf16[2,1076,576]{1,2,0:T(8,128)(2,1)} %param.30), kind=kOutput, calls=%fused_computation.99 | convolution fusion | flops 5476090880 | bytes 16323536 | tf_op jit(solution)/shard_map/bnf,fw->bnw/dot_general | solution.py:48
  1373.3 98.5 %all-reduce.21.cloned.1.call-done = bf16[6,729,576]{1,2,0:T(8,128)(2,1)} async-done(((bf16[6,729,576]{1,2,0:T(8,128)(2,1)}), bf16[6,729,576]{1,2,0:T(8,128)(2,1)}) %all-reduce.21.cloned.1.call-update) | async-done | bytes 5038864 | tf_op jit(solution)/shard_map/psum | solution.py:49
  1471.8 8.4 fusion.55
  (74 shorter events, 2.3 us)
Async XLA Ops:
  6.5 215.1 %all-reduce.25.cloned.1.call-start = ((), (), s32[]{:S(2)}) async-start(), calls=%async_computation.7 | async-start | bytes 15925248 | tf_op jit(solution)/shard_map/psum | solution.py:36
  10.6 18.9 %slice-start = ((s8[5308416]{0:T(1024)(128)(4,1)}), s8[1114112]{0:T(1024)(128)(4,1)S(1)}, s32[]{:S(2)}) async-start(s8[5308416]{0:T(1024)(128)(4,1)} %bitcast.142), calls=%async_computation.8 | async-start | bytes 2228224
  22.2 7.3 slice-start.1
  22.2 7.3 copy-start.11
  29.5 4.5 copy-start.12
  34.1 4.8 copy-start.5
  34.1 4.8 copy-start.6
  38.6 329.7 %all-reduce.11.cloned.1.call-start = ((), (), s32[]{:S(2)}) async-start(), calls=%async_computation | async-start | bytes 10616832 | tf_op jit(solution)/shard_map/psum | solution.py:43
  221.7 25.7 %copy-start.13 = (bf16[2,4,72,576]{3,2,1,0:T(8,128)(2,1)S(1)}, bf16[2,4,72,576]{3,2,1,0:T(8,128)(2,1)}, u32[]{:S(2)}) copy-start(bf16[2,4,72,576]{3,2,1,0:T(8,128)(2,1)} %param.24) | copy-start | bytes 1990660
  247.4 22.9 %copy-start.1 = (f32[2,576]{1,0:T(2,128)S(1)}, f32[2,576]{1,0:T(2,128)}, u32[]{:S(2)}) copy-start(f32[2,576]{1,0:T(2,128)} %param.25) | copy-start | bytes 13828
  247.4 23.0 %copy-start.3 = (f32[2,576]{1,0:T(2,128)S(1)}, f32[2,576]{1,0:T(2,128)}, u32[]{:S(2)}) copy-start(f32[2,576]{1,0:T(2,128)} %param.27) | copy-start | bytes 13828
  247.4 23.0 %copy-start.4 = (f32[2,576]{1,0:T(2,128)S(1)}, f32[2,576]{1,0:T(2,128)}, u32[]{:S(2)}) copy-start(f32[2,576]{1,0:T(2,128)} %param.26) | copy-start | bytes 13828
  270.3 354.3 %all-reduce.13.cloned.1.call-start = ((), (), s32[]{:S(2)}) async-start(), calls=%async_computation.1 | async-start | bytes 19906560 | tf_op jit(solution)/shard_map/psum | solution.py:47
  386.1 13.4 copy-start
  399.4 339.3 %all-reduce.15.cloned.1.call-start = ((), (), s32[]{:S(2)}) async-start(), calls=%async_computation.2 | async-start | bytes 10616832 | tf_op jit(solution)/shard_map/psum | solution.py:49
  624.6 15.6 %copy-start.2 = (f32[2,576]{1,0:T(2,128)S(1)}, f32[2,576]{1,0:T(2,128)}, u32[]{:S(2)}) copy-start(f32[2,576]{1,0:T(2,128)} %param.31) | copy-start | bytes 13828
  640.1 116.2 %copy-start.10 = (bf16[2,576,4,72]{1,3,2,0:T(8,128)(2,1)S(1)}, bf16[2,576,4,72]{1,3,2,0:T(8,128)(2,1)}, u32[]{:S(2)}) copy-start(bf16[2,576,4,72]{1,3,2,0:T(8,128)(2,1)} %param.19) | copy-start | bytes 1990660
  640.1 314.8 %all-reduce.23.cloned.1.call-start = ((), (), s32[]{:S(2)}) async-start(), calls=%async_computation.6 | async-start | bytes 15925248 | tf_op jit(solution)/shard_map/psum | solution.py:36
  747.2 16.3 %slice-start.2 = ((s8[5308416]{0:T(1024)(128)(4,1)}), s8[1114112]{0:T(1024)(128)(4,1)S(1)}, s32[]{:S(2)}) async-start(s8[5308416]{0:T(1024)(128)(4,1)} %bitcast.144), calls=%async_computation.10 | async-start | bytes 2228224
  756.4 7.2 slice-start.3
  772.6 328.9 %all-reduce.17.cloned.1.call-start = ((), (), s32[]{:S(2)}) async-start(), calls=%async_computation.3 | async-start | bytes 10616832 | tf_op jit(solution)/shard_map/psum | solution.py:43
  954.9 25.7 %copy-start.9 = (f32[4,72]{1,0:T(4,128)S(1)}, f32[4,72]{1,0:T(4,128)}, u32[]{:S(2)}) copy-start(f32[4,72]{1,0:T(4,128)} %get-tuple-element.36) | copy-start | bytes 3460
  954.9 25.7 %copy-start.14 = (bf16[2,4,72,576]{3,2,1,0:T(8,128)(2,1)S(1)}, bf16[2,4,72,576]{3,2,1,0:T(8,128)(2,1)}, u32[]{:S(2)}) copy-start(bf16[2,4,72,576]{3,2,1,0:T(8,128)(2,1)} %param.24) | copy-start | bytes 1990660
  1003.5 115.7 %copy-start.7 = (f32[576]{0:T(1024)S(1)}, f32[576]{0:T(1024)}, u32[]{:S(2)}) copy-start(f32[576]{0:T(1024)} %get-tuple-element.19) | copy-start | bytes 6916
  1003.5 115.7 %copy-start.8 = (f32[576]{0:T(1024)S(1)}, f32[576]{0:T(1024)}, u32[]{:S(2)}) copy-start(f32[576]{0:T(1024)} %get-tuple-element.47) | copy-start | bytes 6916
  1003.5 354.2 %all-reduce.19.cloned.1.call-start = ((), (), s32[]{:S(2)}) async-start(), calls=%async_computation.4 | async-start | bytes 19906560 | tf_op jit(solution)/shard_map/psum | solution.py:47
  1132.5 339.3 %all-reduce.21.cloned.1.call-start = ((), (), s32[]{:S(2)}) async-start(), calls=%async_computation.5 | async-start | bytes 10616832 | tf_op jit(solution)/shard_map/psum | solution.py:49
Sparse Core Ops, SparseCore 0:
  38.7 182.8 all-reduce.24
  270.4 97.8 all-reduce.10
  399.5 225.0 all-reduce.12
  640.3 98.3 all-reduce.14
  772.7 182.1 all-reduce.22
  1003.7 97.8 all-reduce.16
  1132.7 225.0 all-reduce.18
  1373.4 98.3 all-reduce.20
where the time goes:
time: 1500 us; the launch traced here: 1490 us
  waiting for transfers between devices  1210 us (81%)
  matrix products  187 us (12%)
  other arithmetic  38.2 us (3%)
  blocking collectives  38 us (3%)
    psum x2, waiting for transfers between devices, local_fn(): lax.psum(part_up, 'tx').astype(jnp.float32) + b_up[layer]  450 us
    psum x2, waiting for transfers between devices, local_fn(): sum_q, k_proj, sum_v = lax.psum((part_q, part_k, part_v), 'tx')  364 us
    psum x2, waiting for transfers between devices, local_fn(): lax.psum(part_down, 'ty').astype(jnp.float32)  197 us
    psum x2, waiting for transfers between devices, local_fn(): lax.psum(part_o, 'ty').astype(jnp.float32)  195 us
    sub x2, matrix products, local_fn(): attn_prob = jax.nn.softmax(scores, axis=-1).astype(jnp.bfloat16)  51.4 us
    dot_general x2, matrix products, local_fn(): jnp.einsum('bqhd,hdw->bqw', attended, w_o[layer], preferred_element_type=...  45.7 us
    psum x4, blocking collectives, split_norm(): lax.psum(jnp.stack([jnp.sum(x_f, axis=-1), jnp.sum(x_f * x_f, axis=-1)]),...  38 us
    dot_general x2, matrix products, local_fn(): jnp.einsum('bnf,fw->bnw', hidden, w_down[layer], preferred_element_type=j...  31.1 us
  transfers between devices with their start and end apart: 8, of which 8 were waited for; matrix products, arithmetic and copies ran while one was open for 0% of the time, Pallas kernels for 0%

commit v1 on v0

v1 whole, which is shorter than its diff:
```python
import jax
import jax.numpy as jnp
from jax import lax
from jax.sharding import PartitionSpec as P

EPS = 1e-6
CORE = [(0, 1), (1, 0), (2, 3), (3, 2)]
CHIP = [(0, 2), (2, 0), (1, 3), (3, 1)]
ROW = [(0, 1), (1, 0)]


def norm(x_f, gain, shift):
    mean = jnp.mean(x_f, axis=-1, keepdims=True)
    centred = x_f - mean
    variance = jnp.mean(centred * centred, axis=-1, keepdims=True)
    return (centred * lax.rsqrt(variance + EPS) * gain + shift).astype(jnp.bfloat16)


def pair_order(own, other, index, axis):
    first = jnp.where(index == 0, own, other)
    second = jnp.where(index == 0, other, own)
    return jnp.concatenate([first, second], axis=axis)


def all_reduce(part):
    rows, width = part.shape
    ty = lax.axis_index("ty")
    core, chip = ty % 2, ty // 2
    padded = -(-rows // 32) * 32
    part = jnp.pad(part, ((0, padded - rows), (0, 0)))

    def scatter(value, index, pairs):
        halves = value.reshape(2, value.shape[0] // 2, width)
        got = lax.ppermute(lax.dynamic_index_in_dim(halves, 1 - index, 0, False), "ty", pairs)
        kept = lax.dynamic_index_in_dim(halves, index, 0, False)
        return (kept.astype(jnp.float32) + got.astype(jnp.float32)).astype(jnp.bfloat16)

    quarter = scatter(scatter(part, core, CORE), chip, CHIP)
    half = pair_order(quarter, lax.ppermute(quarter, "ty", CHIP), chip, 0)
    whole = pair_order(half, lax.ppermute(half, "ty", CORE), core, 0)
    return whole[:rows].astype(jnp.float32)


def solution(mesh):
    act_spec = P("dp", None, "tx")
    vec_tx = P(None, "tx")
    proj_spec = P(None, "tx", "ty", None)
    head_vec = P(None, "ty", None)
    in_specs = (act_spec, vec_tx, vec_tx, proj_spec, head_vec, proj_spec, proj_spec, head_vec,
                P(None, "ty", None, "tx"), vec_tx, vec_tx, vec_tx,
                P(None, "tx", "ty"), P(None, "ty"), P(None, "ty", "tx"), vec_tx)

    def local_fn(x_in, ln1_gain, ln1_bias, w_q, b_q, w_k, w_v, b_v, w_o, b_o, ln2_gain, ln2_bias, w_up, b_up, w_down, b_down):
        layers, half_w, heads, head = w_q.shape
        images = x_in.shape[0] // 2
        tx = lax.axis_index("tx")
        scale = head ** -0.5
        dot = lambda a, b: jnp.dot(a, b, preferred_element_type=jnp.float32)

        mine = lax.dynamic_slice_in_dim(x_in, tx * images, images)
        other = lax.ppermute(lax.dynamic_slice_in_dim(x_in, (1 - tx) * images, images), "tx", ROW)
        x_full = pair_order(mine, other, tx, 2)
        vecs = jnp.stack([ln1_gain, ln1_bias, b_o, ln2_gain, ln2_bias, b_down])
        vecs = lax.all_gather(vecs, "tx", axis=2, tiled=True)
        qkv = jnp.concatenate([w.reshape(layers, half_w, heads * head) for w in (w_q, w_k, w_v)], axis=2)
        b_qkv = jnp.concatenate([b_q.reshape(layers, -1), jnp.zeros_like(b_q).reshape(layers, -1), b_v.reshape(layers, -1)], axis=1)
        o_mat = w_o.reshape(layers, heads * head, half_w)

        def gather(w, axis):
            got = lax.ppermute(w, "tx", ROW)
            return pair_order(w, got, tx, axis)

        xs = [x_full[i] for i in range(images)]
        for layer in range(layers):
            g1, s1, bo, g2, s2, bd = [vecs[j, layer] for j in range(6)]
            wqkv = gather(qkv[layer], 0)
            wo = gather(o_mat[layer], 1)
            wup = gather(w_up[layer], 0)
            wdn = gather(w_down[layer], 1)
            mids = []
            for i in range(images):
                normed = norm(xs[i].astype(jnp.float32), g1, s1)
                proj = (dot(normed, wqkv) + b_qkv[layer]).astype(jnp.bfloat16)
                proj = proj.reshape(-1, 3, heads, head)
                scores = jnp.einsum("qhd,khd->hqk", proj[:, 0], proj[:, 1], preferred_element_type=jnp.float32) * scale
                prob = jax.nn.softmax(scores, axis=-1).astype(jnp.bfloat16)
                att = jnp.einsum("hqk,khd->qhd", prob, proj[:, 2], preferred_element_type=jnp.float32).astype(jnp.bfloat16)
                part = dot(att.reshape(-1, heads * head), wo).astype(jnp.bfloat16)
                mids.append((xs[i].astype(jnp.float32) + all_reduce(part) + bo).astype(jnp.bfloat16))
            xs = []
            for i in range(images):
                normed = norm(mids[i].astype(jnp.float32), g2, s2)
                hidden = jax.nn.gelu(dot(normed, wup) + b_up[layer], approximate=True).astype(jnp.bfloat16)
                part = dot(hidden, wdn).astype(jnp.bfloat16)
                xs.append((mids[i].astype(jnp.float32) + all_reduce(part) + bd).astype(jnp.bfloat16))
        y_full = jnp.stack(xs).reshape(images, -1, 2, half_w)
        keep = lax.dynamic_index_in_dim(y_full, tx, 2, False)
        got = lax.ppermute(lax.dynamic_index_in_dim(y_full, 1 - tx, 2, False), "tx", ROW)
        return pair_order(keep, got, tx, 0)

    return jax.shard_map(local_fn, mesh=mesh, in_specs=in_specs, out_specs=act_spec, check_vma=False)
```

time: 1500 us -> 920 us (0.61)
  waiting for transfers between devices: 1210 us -> 351 us
  local copies, waits for them, and re-layouts: 2.19 us -> 167 us
  blocking collectives: 38 us -> 107 us
  starting transfers between devices: 0.72 us -> 44.2 us
  other arithmetic: 38.2 us -> 73.6 us
  matrix products: 187 us -> 162 us
    psum x8 -> x0, waiting for transfers between devices: 1210 us -> none  [the longest x2 450 us: local_fn(): lax.psum(part_up, 'tx').astype(jnp.float32) + b_up[layer]]
    ppermute x0 -> x58, waiting for transfers between devices: none -> 351 us  [the longest x12 100 us: all_reduce(): half = pair_order(quarter, lax.ppermute(quarter, 'ty', CHIP), chip, 0)]
    all_gather x0 -> x1, blocking collectives: none -> 107 us  [local_fn(): vecs = lax.all_gather(vecs, 'tx', axis=2, tiled=True)]
    slice x4 -> x3, local copies, waits for them, and re-layouts: 1.48 us -> 51.9 us  [the longest x1 50.1 us: local_fn(): g1, s1, bo, g2, s2, bd = [vecs[j, layer] for j in range(6)]]
    ppermute x0 -> x58, starting transfers between devices: none -> 44.2 us  [the longest x24 15.9 us: scatter(): lax.ppermute(lax.dynamic_index_in_dim(halves, 1 - index, 0, False), 'ty',...]
    psum x4 -> x0, blocking collectives: 38 us -> none  [split_norm(): lax.psum(jnp.stack([jnp.sum(x_f, axis=-1), jnp.sum(x_f * x_f, axis=-1)]),...]
    squeeze x0 -> x31, local copies, waits for them, and re-layouts: none -> 25.8 us  [the longest x24 8.63 us: scatter(): lax.dynamic_index_in_dim(halves, 1 - index, 0, False)]
    convert_element_type x0 -> x9, local copies, waits for them, and re-layouts: none -> 25.2 us  [the longest x6 16.2 us: local_fn(): proj = (dot(normed, wqkv) + b_qkv[layer]).astype(jnp.bfloat16)]
  transfers between devices with their start and end apart: 8 -> 58, of which waited for: 8 -> 32; matrix products, arithmetic and copies ran while one was open for 0% -> 28% of each run, Pallas kernels for 0% -> 0%
where the time goes in v1:
time: 920 us; the launch traced here: 908 us
  waiting for transfers between devices  351 us (38%)
  local copies, waits for them, and re-layouts  167 us (18%)
  matrix products  162 us (18%)
  blocking collectives  107 us (12%)
  other arithmetic  73.6 us (8%)
  starting transfers between devices  44.2 us (5%)
    all_gather x1, blocking collectives, local_fn(): vecs = lax.all_gather(vecs, 'tx', axis=2, tiled=True)  107 us
    ppermute x12, waiting for transfers between devices, all_reduce(): half = pair_order(quarter, lax.ppermute(quarter, 'ty', CHIP), chip, 0)  100 us
    ppermute x8, waiting for transfers between devices, gather(): got = lax.ppermute(w, 'tx', ROW)  97.4 us
    ppermute x24, waiting for transfers between devices, scatter(): lax.ppermute(lax.dynamic_index_in_dim(halves, 1 - index, 0, False), 'ty',...  93.1 us
    dot_general x18, matrix products, local_fn(): dot = lambda a, b: jnp.dot(a, b, preferred_element_type=jnp.float32)  88.9 us
    ppermute x1, waiting for transfers between devices, local_fn(): lax.ppermute(lax.dynamic_index_in_dim(y_full, 1 - tx, 2, False), 'tx', ROW)  54.4 us
    slice x1, local copies, waits for them, and re-layouts, local_fn(): g1, s1, bo, g2, s2, bd = [vecs[j, layer] for j in range(6)]  50.1 us
    sub x6, matrix products, local_fn(): prob = jax.nn.softmax(scores, axis=-1).astype(jnp.bfloat16)  45.2 us
  transfers between devices with their start and end apart: 58, of which 32 were waited for; matrix products, arithmetic and copies ran while one was open for 28% of the time, Pallas kernels for 0%

profile of v1, /device:TPU:0, one launch (start us, length us, event | category | flops | bytes accessed | tf_op | source)
XLA Modules:
  0.0 908.2 jit_solution(3492798956793716822)
XLA Ops:
  23.8 107.3 %all_gather.3 = f32[6,2,1152]{0,1,2:T(2,128)S(1)} all-gather(f32[6,2,576]{0,1,2:T(2,128)S(1)} %copy.115), channel_id=1, replica_groups=mesh['dp'=1,'tx'=2,'ty'=4] {'tx'}, dimensions={2}, use_global_device_ids=true | all-gather | bytes 82944 | tf_op jit(solution)/shard_map/all_gather | solution.py:64
  131.1 50.1 %slice_reduce_fusion = (f32[1152]{0:T(1024)}, f32[1152]{0:T(1024)}, f32[1152]{0:T(1024)}, f32[1152]{0:T(1024)}, f32[1152]{0:T(1024)}, /*index=5*/f32[1152]{0:T(1...) fusion(f32[6,2,1152]{0,1,2:T(2,128)S(1)} %all_gather.3), kind=kLoop, calls=%fused_computation.471 | loop fusion | bytes 110592 | tf_op jit(solution)/shard_map/slice | solution.py:75
  216.9 70.1 %collective-permute-done.20 = bf16[1076,576]{0,1:T(8,128)(2,1)} collective-permute-done((bf16[1076,576]{0,1:T(8,128)(2,1)}, bf16[1076,576]{0,1:T(8,128)(2,1)}, u32[]{:S(2)}, u32[]{:S(2)}) %collective-permute-start.20) | collective-permute-done | bytes 1239584 | tf_op jit(solution)/shard_map/ppermute | solution.py:70
  287.0 25.9 %collective-permute-done.8 = bf16[1076,576]{0,1:T(8,128)(2,1)} collective-permute-done((bf16[1076,576]{0,1:T(8,128)(2,1)}, bf16[1076,576]{0,1:T(8,128)(2,1)}, u32[]{:S(2)}, u32[]{:S(2)}) %collective-permute-start.8) | collective-permute-done | bytes 1239584 | tf_op jit(solution)/shard_map/ppermute | solution.py:70
  413.2 7.8 collective-permute-done.26
  422.3 7.8 collective-permute-done.4
  431.4 7.8 collective-permute-done.43
  439.4 8.9 collective-permute-done.27
  448.5 8.4 collective-permute-done.5
  465.2 10.8 %convolution_convert_fusion.2 = bf16[729,1152]{1,0:T(8,128)(2,1)} fusion(bf16[1076,576]{0,1:T(8,128)(2,1)} %get-tuple-element.73, bf16[1076,576]{0,1:T(8,128)(2,1)} %get-tuple-element.74, bf16[729,1152]{1,0:T(8,128)(2,1)} %copy-done.13, f32[729]{0:T(1024)S(1)} %add_rsqrt_fusion.2, f32[729]{0:T(1024)S(1)} %broadcast_multiply_fusion.2, ...), kind=kOutput, calls=%fused_computation.197 | convolution fusion | flops 3638172672 | bytes 8336792 | tf_op jit(solution)/shard_map/dot_general | solution.py:58
  479.4 10.8 %convolution_convert_fusion.6 = bf16[729,1152]{1,0:T(8,128)(2,1)} fusion(bf16[1076,576]{0,1:T(8,128)(2,1)} %get-tuple-element.73, bf16[1076,576]{0,1:T(8,128)(2,1)} %get-tuple-element.74, bf16[729,1152]{1,0:T(8,128)(2,1)S(1)} %copy-done.11, f32[729]{0:T(1024)S(1)} %add_rsqrt_fusion.6, f32[729]{0:T(1024)S(1)} %broadcast_multiply_fusion.6, ...), kind=kOutput, calls=%fused_computation.201 | convolution fusion | flops 3638172672 | bytes 8336792 | tf_op jit(solution)/shard_map/dot_general | solution.py:58
  495.1 10.4 %convolution_convert_fusion.10 = bf16[729,1152]{1,0:T(8,128)(2,1)} fusion(bf16[1076,576]{0,1:T(8,128)(2,1)} %get-tuple-element.73, bf16[1076,576]{0,1:T(8,128)(2,1)} %get-tuple-element.74, bf16[729,1152]{1,0:T(8,128)(2,1)S(1)} %copy-done.9, f32[1152]{0:T(1024)S(1)} %copy-done.65, f32[1152]{0:T(1024)S(1)} %copy-done.66, f32[729]{0:T(1024)S(1)} %add_rsqrt_fusion.10, ...), kind=kOutput, calls=%fused_computation.205 | convolution fusion | flops 3638172672 | bytes 8336792 | tf_op jit(solution)/shard_map/dot_general | solution.py:58
  522.8 7.8 collective-permute-done.30
  531.9 7.8 collective-permute-done.10
  541.0 7.8 collective-permute-done.47
  548.9 8.9 collective-permute-done.31
  558.0 8.2 collective-permute-done.11
  654.3 7.8 collective-permute-done.34
  663.3 7.8 collective-permute-done.16
  672.4 7.8 collective-permute-done.51
  680.4 8.9 collective-permute-done.35
  689.5 8.4 collective-permute-done.17
  706.2 9.6 %convolution_convert_fusion = bf16[729,1152]{1,0:T(8,128)(2,1)S(1)} fusion(bf16[1076,576]{0,1:T(8,128)(2,1)} %get-tuple-element.60, bf16[1076,576]{0,1:T(8,128)(2,1)} %get-tuple-element.59, bf16[729,1152]{1,0:T(8,128)(2,1)} %copy-done.7, f32[729]{0:T(1024)S(1)} %add_rsqrt_fusion, f32[729]{0:T(1024)S(1)} %broadcast_multiply_fusion, ...), kind=kOutput, calls=%fused_computation.195 | convolution fusion | flops 3638172672 | bytes 8336792 | tf_op jit(solution)/shard_map/dot_general | solution.py:58
  718.9 10.3 %convolution_convert_fusion.4 = bf16[729,1152]{1,0:T(8,128)(2,1)} fusion(bf16[1076,576]{0,1:T(8,128)(2,1)} %get-tuple-element.60, bf16[1076,576]{0,1:T(8,128)(2,1)} %get-tuple-element.59, bf16[729,1152]{1,0:T(8,128)(2,1)S(1)} %copy-done.6, f32[729]{0:T(1024)S(1)} %add_rsqrt_fusion.4, f32[729]{0:T(1024)S(1)} %broadcast_multiply_fusion.4, ...), kind=kOutput, calls=%fused_computation.199 | convolution fusion | flops 3638172672 | bytes 8336792 | tf_op jit(solution)/shard_map/dot_general | solution.py:58
  734.1 10.4 %convolution_convert_fusion.8 = bf16[729,1152]{1,0:T(8,128)(2,1)} fusion(bf16[1076,576]{0,1:T(8,128)(2,1)} %get-tuple-element.60, bf16[1076,576]{0,1:T(8,128)(2,1)} %get-tuple-element.59, bf16[729,1152]{1,0:T(8,128)(2,1)S(1)} %copy-done.5, f32[1152]{0:T(1024)S(1)} %copy-done.61, f32[1152]{0:T(1024)S(1)} %copy-done.62, f32[729]{0:T(1024)S(1)} %add_rsqrt_fusion.8, ...), kind=kOutput, calls=%fused_computation.203 | convolution fusion | flops 3638172672 | bytes 8336792 | tf_op jit(solution)/shard_map/dot_general | solution.py:58
  762.0 7.8 collective-permute-done.38
  771.1 7.8 collective-permute-done.22
  780.2 7.8 collective-permute-done.55
  788.1 8.9 collective-permute-done.39
  797.2 8.2 collective-permute-done.23
  833.9 54.4 %collective-permute-done.57 = bf16[3,729,576]{1,2,0:T(8,128)(2,1)} collective-permute-done((bf16[3,729,576]{1,2,0:T(8,128)(2,1)}, bf16[3,729,576]{1,2,0:T(8,128)(2,1)}, u32[]{:S(2)}, u32[]{:S(2)}) %collective-permute-start.57) | collective-permute-done | bytes 2519456 | tf_op jit(solution)/shard_map/ppermute | solution.py:98
  899.1 8.7 copy.141
  (462 shorter events, 365.0 us)
Async XLA Ops:
  5.3 197.2 %collective-permute-start.1 = (bf16[576,864]{1,0:T(8,128)(2,1)}, bf16[576,864]{1,0:T(8,128)(2,1)}, u32[]{:S(2)}, u32[]{:S(2)}) collective-permute-start(bf16[576,864]{1,0:T(8,128)(2,1)} %copy.116), channel_id=1, source_target_pairs={{0,4},{4,0},{1,5},{5,1},{2,6},{6,2},{3,7},{7,3}} | collective-permute-start | bytes 2985992 | tf_op jit(solution)/shard_map/ppermute | solution.py:70
  10.4 194.6 %collective-permute-start.13 = (bf16[576,864]{1,0:T(8,128)(2,1)}, bf16[576,864]{1,0:T(8,128)(2,1)}, u32[]{:S(2)}, u32[]{:S(2)}) collective-permute-start(bf16[576,864]{1,0:T(8,128)(2,1)} %copy.121), channel_id=1, source_target_pairs={{0,4},{4,0},{1,5},{5,1},{2,6},{6,2},{3,7},{7,3}} | collective-permute-start | bytes 2985992 | tf_op jit(solution)/shard_map/ppermute | solution.py:70
  11.7 176.7 %collective-permute-start.2 = (bf16[288,576]{1,0:T(8,128)(2,1)S(1)}, bf16[288,576]{1,0:T(8,128)(2,1)}, u32[]{:S(2)}, u32[]{:S(2)}) collective-permute-start(bf16[288,576]{1,0:T(8,128)(2,1)S(1)} %bitcast.518), channel_id=1, source_target_pairs={{0,4},{4,0},{1,5},{5,1},{2,6},{6,2},{3,7},{7,3}} | collective-permute-start | bytes 995336 | tf_op jit(solution)/shard_map/ppermute | solution.py:70
  17.1 195.3 %collective-permute-start.19 = (bf16[576,1076]{1,0:T(8,128)(2,1)}, bf16[576,1076]{1,0:T(8,128)(2,1)}, u32[]{:S(2)}, u32[]{:S(2)}) collective-permute-start(bf16[576,1076]{1,0:T(8,128)(2,1)} %get-tuple-element.71), channel_id=1, source_target_pairs={{0,4},{4,0},{1,5},{5,1},{2,6},{6,2},{3,7},{7,3}} | collective-permute-start | bytes 3718664 | tf_op jit(solution)/shard_map/ppermute | solution.py:70
  17.1 195.3 %collective-permute-start.7 = (bf16[576,1076]{1,0:T(8,128)(2,1)}, bf16[576,1076]{1,0:T(8,128)(2,1)}, u32[]{:S(2)}, u32[]{:S(2)}) collective-permute-start(bf16[576,1076]{1,0:T(8,128)(2,1)} %get-tuple-element.72), channel_id=1, source_target_pairs={{0,4},{4,0},{1,5},{5,1},{2,6},{6,2},{3,7},{7,3}} | collective-permute-start | bytes 3718664 | tf_op jit(solution)/shard_map/ppermute | solution.py:70
  198.1 119.0 %collective-permute-start = (bf16[3,729,576]{1,2,0:T(8,128)(2,1)}, bf16[3,729,576]{1,2,0:T(8,128)(2,1)}, u32[]{:S(2)}, u32[]{:S(2)}) collective-permute-start(bf16[3,729,576]{1,2,0:T(8,128)(2,1)} %get-tuple-element.56), channel_id=1, source_target_pairs={{0,4},{4,0},{1,5},{5,1},{2,6},{6,2},{3,7},{7,3}} | collective-permute-start | bytes 7558280 | tf_op jit(solution)/shard_map/ppermute | solution.py:61
  202.5 84.5 %collective-permute-start.20 = (bf16[1076,576]{0,1:T(8,128)(2,1)}, bf16[1076,576]{0,1:T(8,128)(2,1)}, u32[]{:S(2)}, u32[]{:S(2)}) collective-permute-start(bf16[1076,576]{0,1:T(8,128)(2,1)} %get-tuple-element.75), channel_id=1, source_target_pairs={{0,4},{4,0},{1,5},{5,1},{2,6},{6,2},{3,7},{7,3}} | collective-permute-start | bytes 3718664 | tf_op jit(solution)/shard_map/ppermute | solution.py:70
  205.1 107.8 %collective-permute-start.8 = (bf16[1076,576]{0,1:T(8,128)(2,1)}, bf16[1076,576]{0,1:T(8,128)(2,1)}, u32[]{:S(2)}, u32[]{:S(2)}) collective-permute-start(bf16[1076,576]{0,1:T(8,128)(2,1)} %get-tuple-element.76), channel_id=1, source_target_pairs={{0,4},{4,0},{1,5},{5,1},{2,6},{6,2},{3,7},{7,3}} | collective-permute-start | bytes 3718664 | tf_op jit(solution)/shard_map/ppermute | solution.py:70
  353.7 43.5 %collective-permute-start.41 = (bf16[368,1152]{1,0:T(8,128)(2,1)}, bf16[368,1152]{1,0:T(8,128)(2,1)}, u32[]{:S(2)}, u32[]{:S(2)}) collective-permute-start(bf16[368,1152]{1,0:T(8,128)(2,1)} %dynamic-slice_bitcast_fusion.5), channel_id=1, source_target_pairs={{0,1},{1,0},{2,3},{3,2},{4,5},{5,4},{6,7},{7,6}} | collective-permute-start | bytes 2543624 | tf_op jit(solution)/shard_map/ppermute | solution.py:34
  376.4 24.0 %collective-permute-start.25 = (bf16[368,1152]{1,0:T(8,128)(2,1)}, bf16[368,1152]{1,0:T(8,128)(2,1)}, u32[]{:S(2)}, u32[]{:S(2)}) collective-permute-start(bf16[368,1152]{1,0:T(8,128)(2,1)} %dynamic-slice_bitcast_fusion.9), channel_id=1, source_target_pairs={{0,1},{1,0},{2,3},{3,2},{4,5},{5,4},{6,7},{7,6}} | collective-permute-start | bytes 2543624 | tf_op jit(solution)/shard_map/ppermute | solution.py:34
  401.9 19.1 %collective-permute-start.26 = (bf16[184,1152]{1,0:T(8,128)(2,1)S(1)}, bf16[184,1152]{1,0:T(8,128)(2,1)S(1)}, u32[]{:S(2)}, u32[]{:S(2)}) collective-permute-start(bf16[184,1152]{1,0:T(8,128)(2,1)S(1)} %dynamic-slice_bitcast_fusion.21), channel_id=1, source_target_pairs={{0,2},{2,0},{1,3},{3,1},{4,6},{6,4},{5,7},{7,5}} | collective-permute-start | bytes 1271816 | tf_op jit(solution)/shard_map/ppermute | solution.py:34
  403.1 27.0 %collective-permute-start.4 = (bf16[184,1152]{1,0:T(8,128)(2,1)S(1)}, bf16[184,1152]{1,0:T(8,128)(2,1)S(1)}, u32[]{:S(2)}, u32[]{:S(2)}) collective-permute-start(bf16[184,1152]{1,0:T(8,128)(2,1)S(1)} %dynamic-slice_bitcast_fusion.25), channel_id=1, source_target_pairs={{0,2},{2,0},{1,3},{3,1},{4,6},{6,4},{5,7},{7,5}} | collective-permute-start | bytes 1271816 | tf_op jit(solution)/shard_map/ppermute | solution.py:34
  412.1 27.1 %collective-permute-start.43 = (bf16[184,1152]{1,0:T(8,128)(2,1)S(1)}, bf16[184,1152]{1,0:T(8,128)(2,1)S(1)}, u32[]{:S(2)}, u32[]{:S(2)}) collective-permute-start(bf16[184,1152]{1,0:T(8,128)(2,1)S(1)} %fusion.299), channel_id=1, source_target_pairs={{0,2},{2,0},{1,3},{3,1},{4,6},{6,4},{5,7},{7,5}} | collective-permute-start | bytes 1271816 | tf_op jit(solution)/shard_map/ppermute | solution.py:39
  421.1 27.1 %collective-permute-start.27 = (bf16[184,1152]{1,0:T(8,128)(2,1)S(1)}, bf16[184,1152]{1,0:T(8,128)(2,1)S(1)}, u32[]{:S(2)}, u32[]{:S(2)}) collective-permute-start(bf16[184,1152]{1,0:T(8,128)(2,1)S(1)} %fusion.303), channel_id=1, source_target_pairs={{0,2},{2,0},{1,3},{3,1},{4,6},{6,4},{5,7},{7,5}} | collective-permute-start | bytes 1271816 | tf_op jit(solution)/shard_map/ppermute | solution.py:39
  430.2 26.7 %collective-permute-start.5 = (bf16[184,1152]{1,0:T(8,128)(2,1)S(1)}, bf16[184,1152]{1,0:T(8,128)(2,1)S(1)}, u32[]{:S(2)}, u32[]{:S(2)}) collective-permute-start(bf16[184,1152]{1,0:T(8,128)(2,1)S(1)} %fusion.307), channel_id=1, source_target_pairs={{0,2},{2,0},{1,3},{3,1},{4,6},{6,4},{5,7},{7,5}} | collective-permute-start | bytes 1271816 | tf_op jit(solution)/shard_map/ppermute | solution.py:39
  478.7 28.6 %collective-permute-start.45 = (bf16[368,1152]{1,0:T(8,128)(2,1)}, bf16[368,1152]{1,0:T(8,128)(2,1)}, u32[]{:S(2)}, u32[]{:S(2)}) collective-permute-start(bf16[368,1152]{1,0:T(8,128)(2,1)} %dynamic-slice_bitcast_fusion.4), channel_id=1, source_target_pairs={{0,1},{1,0},{2,3},{3,2},{4,5},{5,4},{6,7},{7,6}} | collective-permute-start | bytes 2543624 | tf_op jit(solution)/shard_map/ppermute | solution.py:34
  512.6 27.0 %collective-permute-start.10 = (bf16[184,1152]{1,0:T(8,128)(2,1)S(1)}, bf16[184,1152]{1,0:T(8,128)(2,1)S(1)}, u32[]{:S(2)}, u32[]{:S(2)}) collective-permute-start(bf16[184,1152]{1,0:T(8,128)(2,1)S(1)} %dynamic-slice_bitcast_fusion.24), channel_id=1, source_target_pairs={{0,2},{2,0},{1,3},{3,1},{4,6},{6,4},{5,7},{7,5}} | collective-permute-start | bytes 1271816 | tf_op jit(solution)/shard_map/ppermute | solution.py:34
  521.6 27.1 %collective-permute-start.47 = (bf16[184,1152]{1,0:T(8,128)(2,1)S(1)}, bf16[184,1152]{1,0:T(8,128)(2,1)S(1)}, u32[]{:S(2)}, u32[]{:S(2)}) collective-permute-start(bf16[184,1152]{1,0:T(8,128)(2,1)S(1)} %fusion.298), channel_id=1, source_target_pairs={{0,2},{2,0},{1,3},{3,1},{4,6},{6,4},{5,7},{7,5}} | collective-permute-start | bytes 1271816 | tf_op jit(solution)/shard_map/ppermute | solution.py:39
  530.7 27.1 %collective-permute-start.31 = (bf16[184,1152]{1,0:T(8,128)(2,1)S(1)}, bf16[184,1152]{1,0:T(8,128)(2,1)S(1)}, u32[]{:S(2)}, u32[]{:S(2)}) collective-permute-start(bf16[184,1152]{1,0:T(8,128)(2,1)S(1)} %fusion.302), channel_id=1, source_target_pairs={{0,2},{2,0},{1,3},{3,1},{4,6},{6,4},{5,7},{7,5}} | collective-permute-start | bytes 1271816 | tf_op jit(solution)/shard_map/ppermute | solution.py:39
  539.8 26.4 %collective-permute-start.11 = (bf16[184,1152]{1,0:T(8,128)(2,1)S(1)}, bf16[184,1152]{1,0:T(8,128)(2,1)S(1)}, u32[]{:S(2)}, u32[]{:S(2)}) collective-permute-start(bf16[184,1152]{1,0:T(8,128)(2,1)S(1)} %fusion.306), channel_id=1, source_target_pairs={{0,2},{2,0},{1,3},{3,1},{4,6},{6,4},{5,7},{7,5}} | collective-permute-start | bytes 1271816 | tf_op jit(solution)/shard_map/ppermute | solution.py:39
  594.4 43.7 %collective-permute-start.49 = (bf16[368,1152]{1,0:T(8,128)(2,1)}, bf16[368,1152]{1,0:T(8,128)(2,1)}, u32[]{:S(2)}, u32[]{:S(2)}) collective-permute-start(bf16[368,1152]{1,0:T(8,128)(2,1)} %dynamic-slice_bitcast_fusion.3), channel_id=1, source_target_pairs={{0,1},{1,0},{2,3},{3,2},{4,5},{5,4},{6,7},{7,6}} | collective-permute-start | bytes 2543624 | tf_op jit(solution)/shard_map/ppermute | solution.py:34
  617.2 24.2 %collective-permute-start.33 = (bf16[368,1152]{1,0:T(8,128)(2,1)}, bf16[368,1152]{1,0:T(8,128)(2,1)}, u32[]{:S(2)}, u32[]{:S(2)}) collective-permute-start(bf16[368,1152]{1,0:T(8,128)(2,1)} %dynamic-slice_bitcast_fusion.7), channel_id=1, source_target_pairs={{0,1},{1,0},{2,3},{3,2},{4,5},{5,4},{6,7},{7,6}} | collective-permute-start | bytes 2543624 | tf_op jit(solution)/shard_map/ppermute | solution.py:34
  644.1 27.0 %collective-permute-start.16 = (bf16[184,1152]{1,0:T(8,128)(2,1)S(1)}, bf16[184,1152]{1,0:T(8,128)(2,1)S(1)}, u32[]{:S(2)}, u32[]{:S(2)}) collective-permute-start(bf16[184,1152]{1,0:T(8,128)(2,1)S(1)} %dynamic-slice_bitcast_fusion.23), channel_id=1, source_target_pairs={{0,2},{2,0},{1,3},{3,1},{4,6},{6,4},{5,7},{7,5}} | collective-permute-start | bytes 1271816 | tf_op jit(solution)/shard_map/ppermute | solution.py:34
  653.1 27.1 %collective-permute-start.51 = (bf16[184,1152]{1,0:T(8,128)(2,1)S(1)}, bf16[184,1152]{1,0:T(8,128)(2,1)S(1)}, u32[]{:S(2)}, u32[]{:S(2)}) collective-permute-start(bf16[184,1152]{1,0:T(8,128)(2,1)S(1)} %fusion.297), channel_id=1, source_target_pairs={{0,2},{2,0},{1,3},{3,1},{4,6},{6,4},{5,7},{7,5}} | collective-permute-start | bytes 1271816 | tf_op jit(solution)/shard_map/ppermute | solution.py:39
  662.2 27.1 %collective-permute-start.35 = (bf16[184,1152]{1,0:T(8,128)(2,1)S(1)}, bf16[184,1152]{1,0:T(8,128)(2,1)S(1)}, u32[]{:S(2)}, u32[]{:S(2)}) collective-permute-start(bf16[184,1152]{1,0:T(8,128)(2,1)S(1)} %fusion.301), channel_id=1, source_target_pairs={{0,2},{2,0},{1,3},{3,1},{4,6},{6,4},{5,7},{7,5}} | collective-permute-start | bytes 1271816 | tf_op jit(solution)/shard_map/ppermute | solution.py:39
  671.3 26.6 %collective-permute-start.17 = (bf16[184,1152]{1,0:T(8,128)(2,1)S(1)}, bf16[184,1152]{1,0:T(8,128)(2,1)S(1)}, u32[]{:S(2)}, u32[]{:S(2)}) collective-permute-start(bf16[184,1152]{1,0:T(8,128)(2,1)S(1)} %fusion.305), channel_id=1, source_target_pairs={{0,2},{2,0},{1,3},{3,1},{4,6},{6,4},{5,7},{7,5}} | collective-permute-start | bytes 1271816 | tf_op jit(solution)/shard_map/ppermute | solution.py:39
  718.1 28.3 %collective-permute-start.53 = (bf16[368,1152]{1,0:T(8,128)(2,1)}, bf16[368,1152]{1,0:T(8,128)(2,1)}, u32[]{:S(2)}, u32[]{:S(2)}) collective-permute-start(bf16[368,1152]{1,0:T(8,128)(2,1)} %dynamic-slice_bitcast_fusion.2), channel_id=1, source_target_pairs={{0,1},{1,0},{2,3},{3,2},{4,5},{5,4},{6,7},{7,6}} | collective-permute-start | bytes 2543624 | tf_op jit(solution)/shard_map/ppermute | solution.py:34
  751.9 27.0 %collective-permute-start.22 = (bf16[184,1152]{1,0:T(8,128)(2,1)S(1)}, bf16[184,1152]{1,0:T(8,128)(2,1)S(1)}, u32[]{:S(2)}, u32[]{:S(2)}) collective-permute-start(bf16[184,1152]{1,0:T(8,128)(2,1)S(1)} %dynamic-slice_bitcast_fusion.22), channel_id=1, source_target_pairs={{0,2},{2,0},{1,3},{3,1},{4,6},{6,4},{5,7},{7,5}} | collective-permute-start | bytes 1271816 | tf_op jit(solution)/shard_map/ppermute | solution.py:34
  760.8 27.1 %collective-permute-start.55 = (bf16[184,1152]{1,0:T(8,128)(2,1)S(1)}, bf16[184,1152]{1,0:T(8,128)(2,1)S(1)}, u32[]{:S(2)}, u32[]{:S(2)}) collective-permute-start(bf16[184,1152]{1,0:T(8,128)(2,1)S(1)} %fusion.296), channel_id=1, source_target_pairs={{0,2},{2,0},{1,3},{3,1},{4,6},{6,4},{5,7},{7,5}} | collective-permute-start | bytes 1271816 | tf_op jit(solution)/shard_map/ppermute | solution.py:39
  769.9 27.1 %collective-permute-start.39 = (bf16[184,1152]{1,0:T(8,128)(2,1)S(1)}, bf16[184,1152]{1,0:T(8,128)(2,1)S(1)}, u32[]{:S(2)}, u32[]{:S(2)}) collective-permute-start(bf16[184,1152]{1,0:T(8,128)(2,1)S(1)} %fusion.300), channel_id=1, source_target_pairs={{0,2},{2,0},{1,3},{3,1},{4,6},{6,4},{5,7},{7,5}} | collective-permute-start | bytes 1271816 | tf_op jit(solution)/shard_map/ppermute | solution.py:39
  779.0 26.4 %collective-permute-start.23 = (bf16[184,1152]{1,0:T(8,128)(2,1)S(1)}, bf16[184,1152]{1,0:T(8,128)(2,1)S(1)}, u32[]{:S(2)}, u32[]{:S(2)}) collective-permute-start(bf16[184,1152]{1,0:T(8,128)(2,1)S(1)} %fusion.304), channel_id=1, source_target_pairs={{0,2},{2,0},{1,3},{3,1},{4,6},{6,4},{5,7},{7,5}} | collective-permute-start | bytes 1271816 | tf_op jit(solution)/shard_map/ppermute | solution.py:39
  828.7 59.6 %collective-permute-start.57 = (bf16[3,729,576]{1,2,0:T(8,128)(2,1)}, bf16[3,729,576]{1,2,0:T(8,128)(2,1)}, u32[]{:S(2)}, u32[]{:S(2)}) collective-permute-start(bf16[3,729,576]{1,2,0:T(8,128)(2,1)} %get-tuple-element.54), channel_id=1, source_target_pairs={{0,4},{4,0},{1,5},{5,1},{2,6},{6,2},{3,7},{7,3}} | collective-permute-start | bytes 7558280 | tf_op jit(solution)/shard_map/ppermute | solution.py:98
  (107 other events, 729.3 us)

commit v2 on v0

v2 whole, which is shorter than its diff:
```python
import functools

import jax
import jax.numpy as jnp
from jax import lax
from jax.experimental import pallas as pl
from jax.experimental.pallas import tpu as pltpu
from jax.sharding import PartitionSpec as P

EPS = 1e-6
MESH = pl.DeviceIdType.MESH
F32, BF16 = jnp.float32, jnp.bfloat16


def tn_dot(a, b):
    return lax.dot_general(a, b, (((0,), (0,)), ((), ())), preferred_element_type=F32)


def nn_dot(a, b):
    return jnp.dot(a, b, preferred_element_type=F32)


def gelu(u):
    return 0.5 * u * (1.0 + jnp.tanh(0.7978845608028654 * (u + 0.044715 * u * u * u)))


def kernel(tokens, x_hbm, vec_hbm, col_hbm, wq_hbm, wk_hbm, wv_hbm, wo_hbm, wup_hbm, wdn_hbm, out_hbm,
           xg, h, part, rd, rs, rr, acc, q3, k3, v3, att, hid, wqkv, wo, wup, wdn, vraw, uraw, vt, ut,
           loc_sem, ws_sem, wr_sem, vec_sem, col_sem, x_sem, en_s, en_r, d2_s, d2_r, rs_s, rs_r, ag_s, ag_r, ex_s, ex_r):
    dp, y, ty = lax.axis_index("dp"), lax.axis_index("tx"), lax.axis_index("ty")
    c, x = ty % 2, ty // 2
    images, width, cols = xg.shape
    half, quarter, eighth = width // 2, width // 4, width // 8
    rows_q = 3 * wq_hbm.shape[1] // 3
    head = v3.shape[1]
    heads = v3.shape[0]
    sib = (dp, y, ty + 1 - 2 * c)
    across = (dp, y, (ty + 2) % 4)
    row = (dp, 1 - y, ty)

    barrier = pltpu.get_barrier_semaphore()
    for peer in (sib, across, row):
        pl.semaphore_signal(barrier, inc=1, device_id=peer, device_id_type=MESH)

    def send(src, dst, ssem, rsem, peer):
        return pltpu.make_async_remote_copy(src_ref=src, dst_ref=dst, send_sem=ssem, recv_sem=rsem,
                                            device_id=peer, device_id_type=MESH)

    def pieces(l):
        res = []
        for t, w in enumerate((wq_hbm, wk_hbm, wv_hbm)):
            res.append((w.at[l], wqkv.at[l, y, pl.ds(rows_q * t, rows_q)]))
        res.append((wo_hbm.at[l], wo.at[l, y]))
        res.append((wup_hbm.at[l], wup.at[l, pl.ds(half * y, half)]))
        res.append((wdn_hbm.at[l], wdn.at[l, pl.ds(half * y, half)]))
        return res

    def w_local(l, n):
        src, dst = pieces(l)[n]
        return pltpu.make_async_copy(src, dst, loc_sem.at[l, n])

    def w_remote(l, n):
        src, dst = pieces(l)[n]
        return send(src, dst, ws_sem.at[l, n], wr_sem.at[l, n], row)

    def w_wait(l, ns):
        for n in ns:
            w_local(l, n).wait()
            w_remote(l, n).wait_recv()

    def mine_in(i):
        return pltpu.make_async_copy(x_hbm.at[y * images + i], xg.at[i, pl.ds(half * y, half)], x_sem.at[i])

    def entry_row(i):
        at = eighth * (2 * c + x)
        return send(x_hbm.at[(1 - y) * images + i, pl.ds(at, eighth)],
                    xg.at[i, pl.ds(half * y + at, eighth)], en_s.at[0, i], en_r.at[0, i], row)

    def entry_fwd(kind, i):
        src_x = x if kind < 3 else 1 - x
        ref = xg.at[i, pl.ds(half * (1 - y) + eighth * (2 * c + src_x), eighth)]
        return send(ref, ref, en_s.at[kind, i], en_r.at[kind, i], across if kind == 1 else sib)

    def entry(i):
        entry_row(i).wait_recv()
        entry_fwd(1, i).start()
        entry_fwd(2, i).start()
        entry_fwd(1, i).wait_recv()
        entry_fwd(3, i).start()

    def entry_done(i):
        mine_in(i).wait()
        entry_fwd(2, i).wait_recv()
        entry_fwd(3, i).wait_recv()
        entry_row(i).wait_send()
        for kind in (1, 2, 3):
            entry_fwd(kind, i).wait_send()

    def d2d(i):
        return send(part.at[pl.ds(half * (1 - c), half)], rd.at[i], d2_s.at[i], d2_r.at[i], sib)

    def scatter(i):
        return send(rs.at[i], rr.at[i], rs_s.at[i], rs_r.at[i], across)

    def gather(kind, i):
        src_x = x if kind < 2 else 1 - x
        ref = xg.at[i, pl.ds(half * c + quarter * src_x, quarter)]
        return send(ref, ref, ag_s.at[kind, i], ag_r.at[kind, i], across if kind == 0 else sib)

    def stage_b(k):
        i = k % images
        d2d(i).wait_recv()
        mine, theirs = quarter * x, quarter * (1 - x)
        acc[i] = (part[pl.ds(pl.multiple_of(half * c + mine, 16), quarter)].astype(F32)
                  + rd[i, pl.ds(pl.multiple_of(mine, 16), quarter)].astype(F32))
        rs[i] = (part[pl.ds(pl.multiple_of(half * c + theirs, 16), quarter)].astype(F32)
                 + rd[i, pl.ds(pl.multiple_of(theirs, 16), quarter)].astype(F32)).astype(BF16)
        scatter(i).start()
        d2d(i).wait_send()

    def column(ref, at, size, lane):
        block = ref[pl.ds(at, size), :]
        picked = jnp.where(lax.broadcasted_iota(jnp.int32, block.shape, 1) == lane, block, 0.0)
        return jnp.sum(picked, axis=1, keepdims=True)

    def out_piece(own_row, i, at_x):
        image = (y if own_row else 1 - y) * images + i
        return out_hbm.at[image, pl.ds(quarter * at_x, quarter)]

    def final_piece(i):
        return xg.at[i, pl.ds(half * c + quarter * x, quarter)]

    def exit_copy(kind, i):
        sems = (ex_s.at[kind, i], ex_r.at[kind, i])
        if kind == 0:
            return send(final_piece(i), out_piece(True, i, x), *sems, row)
        if kind in (1, 2):
            return send(final_piece(i), out_piece(True, i, x), *sems, across if kind == 1 else sib)
        if kind in (3, 4):
            ref = out_piece(False, i, x)
            return send(ref, ref, *sems, across if kind == 3 else sib)
        ref = out_piece(kind == 5, i, 1 - x)
        return send(ref, ref, *sems, sib)

    def exit_local(i):
        return pltpu.make_async_copy(final_piece(i), out_piece(True, i, x), x_sem.at[i])

    def stage_c(k):
        i, s = k % images, k // images
        scatter(i).wait_recv()
        at = pl.multiple_of(half * c + quarter * x, 16)
        bias = column(vt, at, quarter, 8 + s)
        new = xg[i, pl.ds(at, quarter)].astype(F32) + (acc[i] + rr[i].astype(F32)) + bias
        xg[i, pl.ds(at, quarter)] = new.astype(BF16)
        scatter(i).wait_send()

        @pl.when(s < 3)
        def _():
            gather(0, i).start()
            gather(1, i).start()

        @pl.when((s == 3) & (c == y))
        def _():
            exit_copy(1, i).start()
            exit_copy(2, i).start()
            exit_local(i).start()

        @pl.when((s == 3) & (c != y))
        def _():
            exit_copy(0, i).start()

    def stage_d(k):
        i, s = k % images, k // images

        @pl.when(s < 3)
        def _():
            gather(0, i).wait_recv()
            gather(2, i).start()

        @pl.when((s == 3) & (c == y))
        def _():
            send(final_piece(i), out_piece(False, i, x), ex_s.at[0, i], ex_r.at[0, i], row).wait_recv()
            exit_copy(3, i).start()
            exit_copy(4, i).start()
            send(final_piece(i), out_piece(True, i, 1 - x), ex_s.at[1, i], ex_r.at[1, i], across).wait_recv()
            exit_copy(5, i).start()
            piece = out_piece(False, i, 1 - x)
            send(piece, piece, ex_s.at[3, i], ex_r.at[3, i], across).wait_recv()
            exit_copy(6, i).start()

    def gather_done(k):
        i = k % images
        gather(1, i).wait_recv()
        gather(2, i).wait_recv()
        for kind in (0, 1, 2):
            gather(kind, i).wait_send()

    def norm(i, s):
        blocks = [pl.ds(b * quarter, quarter) for b in range(4)]
        total = sum(jnp.sum(xg[i, b].astype(F32), axis=0, keepdims=True) for b in blocks)
        mean = total / width
        spread = jnp.zeros_like(mean)
        for b in blocks:
            d = xg[i, b].astype(F32) - mean
            spread = spread + jnp.sum(d * d, axis=0, keepdims=True)
        inv = lax.rsqrt(spread / width + EPS)
        for n, b in enumerate(blocks):
            gain, shift = column(vt, n * quarter, quarter, s), column(vt, n * quarter, quarter, 4 + s)
            h[b] = ((xg[i, b].astype(F32) - mean) * inv * gain + shift).astype(BF16)

    def project(l, i, make):
        def body(n, _):
            hf = (1 - c) * (1 - n) + c * n
            part[pl.ds(pl.multiple_of(half * hf, 16), half)] = make(hf).astype(BF16)

            @pl.when(n == 0)
            def _():
                d2d(i).start()
            return 0
        lax.fori_loop(0, 2, body, 0)

    factor = (head ** -0.5) * 1.4426950408889634

    def attend(l, i):
        @pl.when(i == 0)
        def _():
            w_wait(l, (0, 1, 2))
        norm(i, 2 * l)
        for t, ref in enumerate((q3, k3, v3)):
            at = pl.ds(rows_q * t, rows_q)
            value = nn_dot(wqkv[l, 0, at], h[:half]) + nn_dot(wqkv[l, 1, at], h[half:])
            value = value + column(ut, rows_q * t, rows_q, l)
            for n in range(heads):
                ref[n, 0:head, :] = value[n * head:(n + 1) * head].astype(BF16)

        def one_head(n, _):
            for start in range(0, cols, 256):
                at = pl.ds(start, 256)
                s = tn_dot(k3[n], q3[n, :, at])
                s = jnp.where(lax.broadcasted_iota(jnp.int32, s.shape, 0) < tokens, s, -1e30)
                e = jnp.exp2((s - jnp.max(s, axis=0, keepdims=True)) * factor)
                p = (e * (1.0 / jnp.sum(e, axis=0, keepdims=True))).astype(BF16)
                att[n, :, at] = nn_dot(v3[n], p)
            return 0
        lax.fori_loop(0, heads, one_head, 0)

        @pl.when(i == 0)
        def _():
            w_wait(l, (3,))
        packed = jnp.concatenate([att[n] for n in range(heads)], axis=0).astype(BF16)
        hid[0:rows_q, :] = packed
        project(l, i, lambda hf: tn_dot(wo[l, hf], hid[0:rows_q, :]))

    def mlp(l, i):
        @pl.when(i == 0)
        def _():
            w_wait(l, (4,))
        norm(i, 2 * l + 1)
        units = wup.shape[2]
        for a in range(0, units, 384):
            b = min(units, a + 384)
            u = tn_dot(wup[l, :, a:b], h[...]) + column(ut, a, b - a, 2 + l)
            hid[a:b, :] = gelu(u).astype(BF16)

        @pl.when(i == 0)
        def _():
            w_wait(l, (5,))
        project(l, i, lambda hf: nn_dot(wdn[l, pl.ds(pl.multiple_of(half * hf, 16), half)], hid[...]))

    for i in range(images):
        mine_in(i).start()
    for n in range(6):
        w_local(0, n).start()
    vec_own = pltpu.make_async_copy(vec_hbm, vraw.at[y, pl.ds(0, 16)], vec_sem.at[0])
    vec_own.start()
    col_own = pltpu.make_async_copy(col_hbm, uraw.at[pl.ds(0, 8)], col_sem)
    col_own.start()
    vec_row = send(vec_hbm, vraw.at[y, pl.ds(0, 16)], vec_sem.at[1], vec_sem.at[2], row)
    pl.semaphore_wait(barrier, 3)
    entry_row(0).start()
    vec_row.start()
    for n in range(3):
        w_remote(0, n).start()
    entry_row(1).start()
    entry_row(2).start()
    for n in range(3, 6):
        w_remote(0, n).start()
    for n in range(6):
        w_local(1, n).start()

    vraw[:, 16:, :] = jnp.zeros((2, vraw.shape[1] - 16, vraw.shape[2]), F32)
    uraw[8:, :] = jnp.zeros((uraw.shape[0] - 8, uraw.shape[1]), F32)
    q3[:, head:, :] = jnp.zeros((heads, q3.shape[1] - head, cols), BF16)
    k3[:, head:, :] = jnp.zeros((heads, k3.shape[1] - head, cols), BF16)
    col_own.wait()
    ut[...] = uraw[...].T
    vec_own.wait()
    vec_row.wait()
    for n in range(2):
        vt[n * half:(n + 1) * half, :] = vraw[n].T[:half]
    entry(0)

    def layer(l, _):
        def attn_step(i, _):
            k = 2 * images * l + i

            @pl.when(l == 0)
            def _():
                entry_done(i)

            @pl.when(l > 0)
            def _():
                gather_done(k)
            attend(l, i)
            stage_b(k)

            @pl.when(k == 0)
            def _():
                for j in range(1, images):
                    entry(j)
                for n in range(6):
                    w_remote(1, n).start()

            @pl.when(k >= 1)
            def _():
                stage_c(k - 1)

            @pl.when(k >= 2)
            def _():
                stage_d(k - 2)
            return 0
        lax.fori_loop(0, images, attn_step, 0)

        def mlp_step(i, _):
            k = 2 * images * l + images + i
            gather_done(k)
            mlp(l, i)
            stage_b(k)
            stage_c(k - 1)
            stage_d(k - 2)
            return 0
        lax.fori_loop(0, images, mlp_step, 0)
        return 0
    lax.fori_loop(0, 2, layer, 0)
    last = 4 * images - 1
    stage_c(last)
    stage_d(last - 1)
    stage_d(last)

    @pl.when(c == y)
    def _():
        for i in range(images):
            exit_local(i).wait()
            for kind in (1, 2, 3, 4, 5, 6):
                exit_copy(kind, i).wait_send()

    @pl.when(c != y)
    def _():
        for i in range(images):
            exit_copy(0, i).wait_send()
            for kind, own_row, at_x in ((2, True, x), (4, False, x), (5, True, 1 - x), (6, False, 1 - x)):
                piece = out_piece(own_row, i, at_x)
                send(piece, piece, ex_s.at[kind, i], ex_r.at[kind, i], sib).wait_recv()
    for l in range(2):
        for n in range(6):
            w_remote(l, n).wait_send()


def solution(mesh):
    act_spec = P("dp", None, "tx")
    vec_tx = P(None, "tx")
    proj_spec = P(None, "tx", "ty", None)
    head_vec = P(None, "ty", None)
    in_specs = (act_spec, vec_tx, vec_tx, proj_spec, head_vec, proj_spec, proj_spec, head_vec,
                P(None, "ty", None, "tx"), vec_tx, vec_tx, vec_tx,
                P(None, "tx", "ty"), P(None, "ty"), P(None, "ty", "tx"), vec_tx)

    def local_fn(x_in, ln1_gain, ln1_bias, w_q, b_q, w_k, w_v, b_v, w_o, b_o, ln2_gain, ln2_bias, w_up, b_up, w_down, b_down):
        total, tokens, half = x_in.shape
        layers, _, heads, head = w_q.shape
        units = w_up.shape[2]
        images, width, rows_q = total // 2, 2 * half, heads * head
        cols = -(-tokens // 256) * 256
        lanes = -(-half // 128) * 128
        long = -(-units // 128) * 128
        flat = lambda w: w.reshape(layers, half, rows_q).transpose(0, 2, 1)
        x_t = jnp.pad(x_in.transpose(0, 2, 1), ((0, 0), (0, 0), (0, cols - tokens)))
        pairs = ((ln1_gain, ln2_gain), (ln1_bias, ln2_bias), (b_o, b_down))
        vec = jnp.concatenate([v[l:l + 1] for a, b in pairs for l in range(layers) for v in (a, b)], axis=0)
        vec = jnp.pad(vec, ((0, 4), (0, lanes - half)))
        qkv_b = jnp.concatenate([b_q.reshape(layers, -1), jnp.zeros((layers, rows_q), F32), b_v.reshape(layers, -1)], axis=1)
        col = jnp.concatenate([jnp.pad(qkv_b, ((0, 0), (0, long - 3 * rows_q))), jnp.pad(b_up, ((0, 0), (0, long - units)))], axis=0)
        col = jnp.pad(col, ((0, 4), (0, 0)))
        dma = pltpu.SemaphoreType.DMA
        vmem = pltpu.VMEM
        y_t = pl.pallas_call(
            functools.partial(kernel, tokens),
            out_shape=jax.ShapeDtypeStruct((total, half, cols), BF16),
            in_specs=[pl.BlockSpec(memory_space=pl.ANY)] * 9,
            out_specs=pl.BlockSpec(memory_space=pl.ANY),
            scratch_shapes=[
                vmem((images, width, cols), BF16), vmem((width, cols), BF16), vmem((width, cols), BF16),
                vmem((images, half, cols), BF16), vmem((images, half // 2, cols), BF16),
                vmem((images, half // 2, cols), BF16), vmem((images, half // 2, cols), F32),
                vmem((heads, 128, cols), BF16), vmem((heads, 128, cols), BF16), vmem((heads, head, cols), BF16),
                vmem((heads, head, cols), F32), vmem((units, cols), BF16),
                vmem((layers, 2, 3 * rows_q, half), BF16), vmem((layers, 2, rows_q, half), BF16),
                vmem((layers, width, units), BF16), vmem((layers, width, units), BF16),
                vmem((2, 128, lanes), F32), vmem((128, long), F32), vmem((width, 128), F32), vmem((long, 128), F32),
                dma((2, 6)), dma((2, 6)), dma((2, 6)), dma((3,)), dma, dma((images,)),
                dma((4, images)), dma((4, images)), dma((images,)), dma((images,)),
                dma((images,)), dma((images,)), dma((3, images)), dma((3, images)),
                dma((7, images)), dma((7, images)),
            ],
            compiler_params=pltpu.CompilerParams(collective_id=0, has_side_effects=True, vmem_limit_bytes=66_000_000),
            name="encoder",
        )(x_t, vec, col, flat(w_q), flat(w_k), flat(w_v), w_o.reshape(layers, rows_q, half), w_up, w_down.transpose(0, 2, 1))
        return y_t[:, :, :tokens].transpose(0, 2, 1)

    return jax.shard_map(local_fn, mesh=mesh, in_specs=in_specs, out_specs=act_spec, check_vma=False)
```

time: 1500 us -> 337 us (0.22)
  waiting for transfers between devices: 1210 us -> 0 us
  Pallas kernels: 0 us -> 320 us
  matrix products: 187 us -> 0 us
  blocking collectives: 38 us -> 0 us
  other arithmetic: 38.2 us -> 0.79 us
    psum x8 -> x0, waiting for transfers between devices: 1210 us -> none  [the longest x2 450 us: local_fn(): lax.psum(part_up, 'tx').astype(jnp.float32) + b_up[layer]]
    pallas_call x0 -> x1, Pallas kernels: none -> 320 us  [local_fn(): pl.pallas_call(functools.partial(kernel, tokens), out_shape=jax.ShapeDtyp...]
    dot_general x12 -> x0, matrix products: 136 us -> none  [the longest x2 45.7 us: local_fn(): jnp.einsum('bqhd,hdw->bqw', attended, w_o[layer], preferred_element_type=...]
    sub x2 -> x0, matrix products: 51.4 us -> none  [local_fn(): attn_prob = jax.nn.softmax(scores, axis=-1).astype(jnp.bfloat16)]
    psum x4 -> x0, blocking collectives: 38 us -> none  [split_norm(): lax.psum(jnp.stack([jnp.sum(x_f, axis=-1), jnp.sum(x_f * x_f, axis=-1)]),...]
    reduce_sum x4 -> x0, other arithmetic: 29.7 us -> none  [split_norm(): jnp.sum(x_f, axis=-1)]
  transfers between devices with their start and end apart: 8 -> 0, of which waited for: 8 -> 0; matrix products, arithmetic and copies ran while one was open for 0% -> 0% of each run, Pallas kernels for 0% -> 0%
where the time goes in v2:
time: 337 us
  Pallas kernels  320 us (95%)
  local copies, waits for them, and re-layouts  15.9 us (5%)
    pallas_call x1, Pallas kernels, local_fn(): pl.pallas_call(functools.partial(kernel, tokens), out_shape=jax.ShapeDtyp...  320 us

profile of v2, /device:TPU:0, one launch (start us, length us, event | category | flops | bytes accessed | tf_op | source)
XLA Modules:
  0.0 336.7 jit_solution(10422487558090721300)
XLA Ops:
  0.0 0.1 pad.28.clone
  0.1 0.8 reshape.18
  0.8 0.8 reshape.19
  1.6 0.1 pad_maximum_fusion
  1.7 0.8 fusion.4
  2.5 0.8 fusion.2
  3.3 0.8 fusion
  4.1 0.1 concatenate.9
  4.1 0.6 pad.21.vec_hbm
  4.8 0.7 select_maximum_fusion
  5.5 0.6 pad.24.col_hbm
  6.1 5.4 %pad.20.x_hbm = bf16[6,576,768]{2,1,0:T(8,128)(2,1)} pad(bf16[6,576,729]{2,1,0:T(8,128)(2,1)} %bitcast.14, bf16[]{:T(256)} %constant.4.clone.1), padding=0_0x0_0x0_39 | pad | bytes 10347266 | tf_op jit(solution)/shard_map/jit(_pad)/pad | solution.py:387
  11.5 320.0 %encoder.1 = bf16[6,576,768]{2,1,0:T(8,128)(2,1)} custom-call(bf16[6,576,768]{2,1,0:T(8,128)(2,1)} %pad.20.x_hbm, f32[16,640]{1,0:T(8,128)} %pad.21.vec_hbm, f32[8,1152]{1,0:T(8,128)} %pad.24.col_hbm, bf16[2,288,576]{2,1,0:T(8,128)(2,1)} %bitcast.16, bf16[2,288,576]{2,1,0:T(8,128)(2,1)} %bitcast.17, bf16[2,288,576]{2,1,0:T(8,128)(2,1)} %bitcast.18, ...), custom_call_target="tpu_custom_call" | custom-call | tf_op jit(solution)/shard_map/encoder/pallas_call | solution.py:396
  331.5 5.2 %slice_bitcast_fusion = bf16[6,729,576]{1,2,0:T(8,128)(2,1)} fusion(bf16[6,576,768]{2,1,0:T(8,128)(2,1)} %encoder.1), kind=kLoop, calls=%fused_computation | loop fusion | bytes 10077696 | tf_op jit(solution)/shard_map/transpose | solution.py:418
  (1 shorter events, 0.0 us)

commit v3 on v2

--- a/solution.py
+++ b/solution.py
@@ -1,5 +1,3 @@
-import functools
-
 import jax
 import jax.numpy as jnp
 from jax import lax
@@ -24,12 +22,13 @@
     return 0.5 * u * (1.0 + jnp.tanh(0.7978845608028654 * (u + 0.044715 * u * u * u)))
 
 
-def kernel(tokens, x_hbm, vec_hbm, col_hbm, wq_hbm, wk_hbm, wv_hbm, wo_hbm, wup_hbm, wdn_hbm, out_hbm,
-           xg, h, part, rd, rs, rr, acc, q3, k3, v3, att, hid, wqkv, wo, wup, wdn, vraw, uraw, vt, ut,
-           loc_sem, ws_sem, wr_sem, vec_sem, col_sem, x_sem, en_s, en_r, d2_s, d2_r, rs_s, rs_r, ag_s, ag_r, ex_s, ex_r):
+def kernel(x_hbm, g1_hbm, g2_hbm, s1_hbm, s2_hbm, bo_hbm, bd_hbm, bq_hbm, bv_hbm, bup_hbm, wq_hbm, wk_hbm, wv_hbm, wo_hbm, wup_hbm, wdn_hbm, out_hbm,
+           xg, h, part, rd, rs, rr, acc, q3, k3, v3, att, hid, wqkv, wo, wup, wdn, vraw, craw, uraw, vpad, cpad, upad, vt, ct, ut,
+           loc_sem, ws_sem, wr_sem, vec_sem, vec_s, vec_r, x_sem, en_s, en_r, d2_s, d2_r, rs_s, rs_r, ag_s, ag_r, ex_s, ex_r):
     dp, y, ty = lax.axis_index("dp"), lax.axis_index("tx"), lax.axis_index("ty")
     c, x = ty % 2, ty // 2
-    images, width, cols = xg.shape
+    images, width, tokens = xg.shape
+    cols = h.shape[1]
     half, quarter, eighth = width // 2, width // 4, width // 8
     rows_q = 3 * wq_hbm.shape[1] // 3
     head = v3.shape[1]
@@ -150,7 +149,7 @@
         scatter(i).wait_recv()
         at = pl.multiple_of(half * c + quarter * x, 16)
         bias = column(vt, at, quarter, 8 + s)
-        new = xg[i, pl.ds(at, quarter)].astype(F32) + (acc[i] + rr[i].astype(F32)) + bias
+        new = xg[i, pl.ds(at, quarter)].astype(F32) + (acc[i] + rr[i].astype(F32))[:, :tokens] + bias
         xg[i, pl.ds(at, quarter)] = new.astype(BF16)
         scatter(i).wait_send()
 
@@ -206,7 +205,7 @@
         inv = lax.rsqrt(spread / width + EPS)
         for n, b in enumerate(blocks):
             gain, shift = column(vt, n * quarter, quarter, s), column(vt, n * quarter, quarter, 4 + s)
-            h[b] = ((xg[i, b].astype(F32) - mean) * inv * gain + shift).astype(BF16)
+            h[b, 0:tokens] = ((xg[i, b].astype(F32) - mean) * inv * gain + shift).astype(BF16)
 
     def project(l, i, make):
         def body(n, _):
@@ -229,9 +228,11 @@
         for t, ref in enumerate((q3, k3, v3)):
             at = pl.ds(rows_q * t, rows_q)
             value = nn_dot(wqkv[l, 0, at], h[:half]) + nn_dot(wqkv[l, 1, at], h[half:])
-            value = value + column(ut, rows_q * t, rows_q, l)
             for n in range(heads):
-                ref[n, 0:head, :] = value[n * head:(n + 1) * head].astype(BF16)
+                one = value[n * head:(n + 1) * head]
+                if t != 1:
+                    one = one + column(ct, 0, head, heads * (t + l) + n)
+                ref[n, 0:head, :] = one.astype(BF16)
 
         def one_head(n, _):
             for start in range(0, cols, 256):
@@ -259,7 +260,7 @@
         units = wup.shape[2]
         for a in range(0, units, 384):
             b = min(units, a + 384)
-            u = tn_dot(wup[l, :, a:b], h[...]) + column(ut, a, b - a, 2 + l)
+            u = tn_dot(wup[l, :, a:b], h[...]) + column(ut, a, b - a, l)
             hid[a:b, :] = gelu(u).astype(BF16)
 
         @pl.when(i == 0)
@@ -271,33 +272,49 @@
         mine_in(i).start()
     for n in range(6):
         w_local(0, n).start()
-    vec_own = pltpu.make_async_copy(vec_hbm, vraw.at[y, pl.ds(0, 16)], vec_sem.at[0])
-    vec_own.start()
-    col_own = pltpu.make_async_copy(col_hbm, uraw.at[pl.ds(0, 8)], col_sem)
-    col_own.start()
-    vec_row = send(vec_hbm, vraw.at[y, pl.ds(0, 16)], vec_sem.at[1], vec_sem.at[2], row)
+    vecs = (g1_hbm, g2_hbm, s1_hbm, s2_hbm, bo_hbm, bd_hbm)
+    small = [pltpu.make_async_copy(v, vraw.at[y, n], vec_sem.at[n]) for n, v in enumerate(vecs)]
+    small += [pltpu.make_async_copy(b, craw.at[n], vec_sem.at[6 + n]) for n, b in enumerate((bq_hbm, bv_hbm))]
+    small.append(pltpu.make_async_copy(bup_hbm, uraw, vec_sem.at[8]))
+    for copy in small:
+        copy.start()
+    vec_row = [send(v, vraw.at[y, n], vec_s.at[n], vec_r.at[n], row) for n, v in enumerate(vecs)]
     pl.semaphore_wait(barrier, 3)
     entry_row(0).start()
-    vec_row.start()
-    for n in range(3):
+    for copy in vec_row:
+        copy.start()
+    for n in range(4):
         w_remote(0, n).start()
-    entry_row(1).start()
-    entry_row(2).start()
-    for n in range(3, 6):
+    for i in range(1, images):
+        entry_row(i).start()
+    for n in range(4, 6):
         w_remote(0, n).start()
     for n in range(6):
         w_local(1, n).start()
 
-    vraw[:, 16:, :] = jnp.zeros((2, vraw.shape[1] - 16, vraw.shape[2]), F32)
-    uraw[8:, :] = jnp.zeros((uraw.shape[0] - 8, uraw.shape[1]), F32)
+    layers = wup.shape[0]
+    for ref in (vpad, cpad, upad):
+        ref[...] = jnp.zeros_like(ref)
+    h[:, cols - 128:] = jnp.zeros((width, 128), BF16)
     q3[:, head:, :] = jnp.zeros((heads, q3.shape[1] - head, cols), BF16)
     k3[:, head:, :] = jnp.zeros((heads, k3.shape[1] - head, cols), BF16)
-    col_own.wait()
-    ut[...] = uraw[...].T
-    vec_own.wait()
-    vec_row.wait()
+    for copy in small:
+        copy.wait()
+    for l in range(layers):
+        upad[l:l + 1, 0:uraw.shape[1]] = uraw[l:l + 1, :]
+        for t in range(2):
+            at = (2 * t + l) * heads
+            cpad[at:at + heads, 0:head] = craw[t, l]
+    ct[...] = cpad[...].T
+    ut[...] = upad[...].T
+    for copy in vec_row:
+        copy.wait()
     for n in range(2):
-        vt[n * half:(n + 1) * half, :] = vraw[n].T[:half]
+        for a in range(6):
+            for l in range(layers):
+                at = 4 * (a // 2) + 2 * l + a % 2
+                vpad[n, at:at + 1, 0:half] = vraw[n, a, l:l + 1, :]
+        vt[n * half:(n + 1) * half, :] = vpad[n].T[:half]
     entry(0)
 
     def layer(l, _):
@@ -333,11 +350,24 @@
 
         def mlp_step(i, _):
             k = 2 * images * l + images + i
+            early = k == images
+
+            @pl.when(early)
+            def _():
+                stage_c(k - 1)
+                stage_d(k - 2)
+                stage_d(k - 1)
             gather_done(k)
             mlp(l, i)
             stage_b(k)
-            stage_c(k - 1)
-            stage_d(k - 2)
+
+            @pl.when(jnp.logical_not(early))
+            def _():
+                stage_c(k - 1)
+
+            @pl.when((k != images) & (k != images + 1))
+            def _():
+                stage_d(k - 2)
             return 0
         lax.fori_loop(0, images, mlp_step, 0)
         return 0
@@ -384,37 +414,33 @@
         lanes = -(-half // 128) * 128
         long = -(-units // 128) * 128
         flat = lambda w: w.reshape(layers, half, rows_q).transpose(0, 2, 1)
-        x_t = jnp.pad(x_in.transpose(0, 2, 1), ((0, 0), (0, 0), (0, cols - tokens)))
-        pairs = ((ln1_gain, ln2_gain), (ln1_bias, ln2_bias), (b_o, b_down))
-        vec = jnp.concatenate([v[l:l + 1] for a, b in pairs for l in range(layers) for v in (a, b)], axis=0)
-        vec = jnp.pad(vec, ((0, 4), (0, lanes - half)))
-        qkv_b = jnp.concatenate([b_q.reshape(layers, -1), jnp.zeros((layers, rows_q), F32), b_v.reshape(layers, -1)], axis=1)
-        col = jnp.concatenate([jnp.pad(qkv_b, ((0, 0), (0, long - 3 * rows_q))), jnp.pad(b_up, ((0, 0), (0, long - units)))], axis=0)
-        col = jnp.pad(col, ((0, 4), (0, 0)))
         dma = pltpu.SemaphoreType.DMA
         vmem = pltpu.VMEM
         y_t = pl.pallas_call(
-            functools.partial(kernel, tokens),
-            out_shape=jax.ShapeDtypeStruct((total, half, cols), BF16),
-            in_specs=[pl.BlockSpec(memory_space=pl.ANY)] * 9,
+            kernel,
+            out_shape=jax.ShapeDtypeStruct((total, half, tokens), BF16),
+            in_specs=[pl.BlockSpec(memory_space=pl.ANY)] * 16,
             out_specs=pl.BlockSpec(memory_space=pl.ANY),
             scratch_shapes=[
-                vmem((images, width, cols), BF16), vmem((width, cols), BF16), vmem((width, cols), BF16),
+                vmem((images, width, tokens), BF16), vmem((width, cols), BF16), vmem((width, cols), BF16),
                 vmem((images, half, cols), BF16), vmem((images, half // 2, cols), BF16),
                 vmem((images, half // 2, cols), BF16), vmem((images, half // 2, cols), F32),
                 vmem((heads, 128, cols), BF16), vmem((heads, 128, cols), BF16), vmem((heads, head, cols), BF16),
                 vmem((heads, head, cols), F32), vmem((units, cols), BF16),
                 vmem((layers, 2, 3 * rows_q, half), BF16), vmem((layers, 2, rows_q, half), BF16),
                 vmem((layers, width, units), BF16), vmem((layers, width, units), BF16),
-                vmem((2, 128, lanes), F32), vmem((128, long), F32), vmem((width, 128), F32), vmem((long, 128), F32),
-                dma((2, 6)), dma((2, 6)), dma((2, 6)), dma((3,)), dma, dma((images,)),
+                vmem((2, 6, layers, half), F32), vmem((2, layers, heads, head), F32), vmem((layers, units), F32),
+                vmem((2, 128, lanes), F32), vmem((128, 128), F32), vmem((128, long), F32),
+                vmem((width, 128), F32), vmem((128, 128), F32), vmem((long, 128), F32),
+                dma((2, 6)), dma((2, 6)), dma((2, 6)), dma((9,)), dma((6,)), dma((6,)), dma((images,)),
                 dma((4, images)), dma((4, images)), dma((images,)), dma((images,)),
                 dma((images,)), dma((images,)), dma((3, images)), dma((3, images)),
                 dma((7, images)), dma((7, images)),
             ],
             compiler_params=pltpu.CompilerParams(collective_id=0, has_side_effects=True, vmem_limit_bytes=66_000_000),
             name="encoder",
-        )(x_t, vec, col, flat(w_q), flat(w_k), flat(w_v), w_o.reshape(layers, rows_q, half), w_up, w_down.transpose(0, 2, 1))
-        return y_t[:, :, :tokens].transpose(0, 2, 1)
+        )(x_in.transpose(0, 2, 1), ln1_gain, ln2_gain, ln1_bias, ln2_bias, b_o, b_down, b_q, b_v, b_up,
+          flat(w_q), flat(w_k), flat(w_v), w_o.reshape(layers, rows_q, half), w_up, w_down.transpose(0, 2, 1))
+        return y_t.transpose(0, 2, 1)
 
     return jax.shard_map(local_fn, mesh=mesh, in_specs=in_specs, out_specs=act_spec, check_vma=False)

time: 337 us -> 329 us (0.976)
  local copies, waits for them, and re-layouts: 15.9 us -> 5.23 us
  Pallas kernels: 320 us -> 324 us
    pad x3 -> x0, local copies, waits for them, and re-layouts: 6.63 us -> none  [the longest x1 5.4 us: local_fn(): x_t = jnp.pad(x_in.transpose(0, 2, 1), ((0, 0), (0, 0), (0, cols - tokens)))]
    transpose x1 -> x0, local copies, waits for them, and re-layouts: 5.23 us -> none  [local_fn(): return y_t[:, :, :tokens].transpose(0, 2, 1)]
    unnamed x0 -> x1, local copies, waits for them, and re-layouts: none -> 5.23 us
    pallas_call x1, Pallas kernels: 320 us -> 324 us  [local_fn(): pl.pallas_call(kernel, out_shape=jax.ShapeDtypeStruct((total, half, token...]
where the time goes in v3:
time: 329 us
  Pallas kernels  324 us (98%)
  local copies, waits for them, and re-layouts  5.23 us (2%)
    pallas_call x1, Pallas kernels, local_fn(): pl.pallas_call(kernel, out_shape=jax.ShapeDtypeStruct((total, half, token...  324 us

profile of v3, /device:TPU:0, one launch (start us, length us, event | category | flops | bytes accessed | tf_op | source)
XLA Modules:
  0.0 329.0 jit_solution(125472343302719713)
XLA Ops:
  0.0 323.8 %encoder.1 = bf16[6,576,729]{2,1,0:T(8,128)(2,1)} custom-call(bf16[6,576,729]{2,1,0:T(8,128)(2,1)} %bitcast.14, f32[2,576]{1,0:T(2,128)} %g1_hbm.1, f32[2,576]{1,0:T(2,128)} %g2_hbm.1, f32[2,576]{1,0:T(2,128)} %s1_hbm.1, f32[2,576]{1,0:T(2,128)} %s2_hbm.1, f32[2,576]{1,0:T(2,128)} %bo_hbm.1, f32[2,576]{1,0:T(2,128)} %bd_hbm.1, f32[2,4,72]{2,1,0:T(4,128)} %bq_hbm.1, ...), custom_call_target="tpu_custom_call" | custom-call | tf_op jit(solution)/shard_map/encoder/pallas_call | solution.py:419
  323.8 5.2 %copy.18 = bf16[6,729,576]{1,2,0:T(8,128)(2,1)} copy(bf16[6,729,576]{1,2,0:T(8,128)(2,1)} %bitcast.13) | data formatting | bytes 10077696

commit v4 on v3

--- a/solution.py
+++ b/solution.py
@@ -221,11 +221,11 @@
     factor = (head ** -0.5) * 1.4426950408889634
 
     def attend(l, i):
-        @pl.when(i == 0)
-        def _():
-            w_wait(l, (0, 1, 2))
         norm(i, 2 * l)
         for t, ref in enumerate((q3, k3, v3)):
+            @pl.when(i == 0)
+            def _():
+                w_wait(l, (t,))
             at = pl.ds(rows_q * t, rows_q)
             value = nn_dot(wqkv[l, 0, at], h[:half]) + nn_dot(wqkv[l, 1, at], h[half:])
             for n in range(heads):
@@ -234,16 +234,18 @@
                     one = one + column(ct, 0, head, heads * (t + l) + n)
                 ref[n, 0:head, :] = one.astype(BF16)
 
+        edge, top = -(-tokens // 16) * 16, tokens // 16 * 16
+
         def one_head(n, _):
-            for start in range(0, cols, 256):
-                at = pl.ds(start, 256)
-                s = tn_dot(k3[n], q3[n, :, at])
-                s = jnp.where(lax.broadcasted_iota(jnp.int32, s.shape, 0) < tokens, s, -1e30)
-                e = jnp.exp2((s - jnp.max(s, axis=0, keepdims=True)) * factor)
-                p = (e * (1.0 / jnp.sum(e, axis=0, keepdims=True))).astype(BF16)
-                att[n, :, at] = nn_dot(v3[n], p)
+            s = nn_dot(k3[n].T[:edge], q3[n])
+            tail = s[top:]
+            tail = jnp.where(lax.broadcasted_iota(jnp.int32, tail.shape, 0) + top < tokens, tail, -1e30)
+            s = jnp.concatenate([s[:top], tail], axis=0)
+            e = jnp.exp2((s - jnp.max(s, axis=0, keepdims=True)) * factor)
+            p = (e * (1.0 / jnp.sum(e, axis=0, keepdims=True))).astype(BF16)
+            att[n] = nn_dot(v3[n, :, :edge], p)
             return 0
-        lax.fori_loop(0, heads, one_head, 0)
+        lax.fori_loop(0, heads, one_head, 0, unroll=2)
 
         @pl.when(i == 0)
         def _():
@@ -253,10 +255,11 @@
         project(l, i, lambda hf: tn_dot(wo[l, hf], hid[0:rows_q, :]))
 
     def mlp(l, i):
+        norm(i, 2 * l + 1)
+
         @pl.when(i == 0)
         def _():
             w_wait(l, (4,))
-        norm(i, 2 * l + 1)
         units = wup.shape[2]
         for a in range(0, units, 384):
             b = min(units, a + 384)
@@ -356,7 +359,6 @@
             def _():
                 stage_c(k - 1)
                 stage_d(k - 2)
-                stage_d(k - 1)
             gather_done(k)
             mlp(l, i)
             stage_b(k)
@@ -365,7 +367,7 @@
             def _():
                 stage_c(k - 1)
 
-            @pl.when((k != images) & (k != images + 1))
+            @pl.when(jnp.logical_not(early))
             def _():
                 stage_d(k - 2)
             return 0

time: 329 us -> 314 us (0.954)
  Pallas kernels: 324 us -> 309 us
    pallas_call x1, Pallas kernels: 324 us -> 309 us  [local_fn(): pl.pallas_call(kernel, out_shape=jax.ShapeDtypeStruct((total, half, token...]
where the time goes in v4:
time: 314 us
  Pallas kernels  309 us (98%)
  local copies, waits for them, and re-layouts  5.23 us (2%)
    pallas_call x1, Pallas kernels, local_fn(): pl.pallas_call(kernel, out_shape=jax.ShapeDtypeStruct((total, half, token...  309 us

profile of v4, /device:TPU:0, one launch (start us, length us, event | category | flops | bytes accessed | tf_op | source)
XLA Modules:
  0.0 314.0 jit_solution(6922012508370583664)
XLA Ops:
  0.0 308.7 %encoder.1 = bf16[6,576,729]{2,1,0:T(8,128)(2,1)} custom-call(bf16[6,576,729]{2,1,0:T(8,128)(2,1)} %bitcast.14, f32[2,576]{1,0:T(2,128)} %g1_hbm.1, f32[2,576]{1,0:T(2,128)} %g2_hbm.1, f32[2,576]{1,0:T(2,128)} %s1_hbm.1, f32[2,576]{1,0:T(2,128)} %s2_hbm.1, f32[2,576]{1,0:T(2,128)} %bo_hbm.1, f32[2,576]{1,0:T(2,128)} %bd_hbm.1, f32[2,4,72]{2,1,0:T(4,128)} %bq_hbm.1, ...), custom_call_target="tpu_custom_call" | custom-call | tf_op jit(solution)/shard_map/encoder/pallas_call | solution.py:421
  308.7 5.2 %copy.18 = bf16[6,729,576]{1,2,0:T(8,128)(2,1)} copy(bf16[6,729,576]{1,2,0:T(8,128)(2,1)} %bitcast.13) | data formatting | bytes 10077696

commit v5 on v4

--- a/solution.py
+++ b/solution.py
@@ -8,6 +8,7 @@
 EPS = 1e-6
 MESH = pl.DeviceIdType.MESH
 F32, BF16 = jnp.float32, jnp.bfloat16
+CUTS = 3
 
 
 def tn_dot(a, b):
@@ -24,7 +25,7 @@
 
 def kernel(x_hbm, g1_hbm, g2_hbm, s1_hbm, s2_hbm, bo_hbm, bd_hbm, bq_hbm, bv_hbm, bup_hbm, wq_hbm, wk_hbm, wv_hbm, wo_hbm, wup_hbm, wdn_hbm, out_hbm,
            xg, h, part, rd, rs, rr, acc, q3, k3, v3, att, hid, wqkv, wo, wup, wdn, vraw, craw, uraw, vpad, cpad, upad, vt, ct, ut,
-           loc_sem, ws_sem, wr_sem, vec_sem, vec_s, vec_r, x_sem, en_s, en_r, d2_s, d2_r, rs_s, rs_r, ag_s, ag_r, ex_s, ex_r):
+           loc_sem, ws_sem, wr_sem, vec_sem, vec_s, vec_r, x_sem, en_s, en_r, d2_s, d2_r, rs_s, rs_r, ag_s, ag_r, ex_s, ex_r, lo_sem):
     dp, y, ty = lax.axis_index("dp"), lax.axis_index("tx"), lax.axis_index("ty")
     c, x = ty % 2, ty // 2
     images, width, tokens = xg.shape
@@ -98,8 +99,11 @@
     def d2d(i):
         return send(part.at[pl.ds(half * (1 - c), half)], rd.at[i], d2_s.at[i], d2_r.at[i], sib)
 
-    def scatter(i):
-        return send(rs.at[i], rr.at[i], rs_s.at[i], rs_r.at[i], across)
+    cut = quarter // CUTS
+
+    def scatter(i, j):
+        at = pl.ds(cut * j, cut)
+        return send(rs.at[i, at], rr.at[i, at], rs_s.at[i, j], rs_r.at[i, j], across)
 
     def gather(kind, i):
         src_x = x if kind < 2 else 1 - x
@@ -114,7 +118,8 @@
                   + rd[i, pl.ds(pl.multiple_of(mine, 16), quarter)].astype(F32))
         rs[i] = (part[pl.ds(pl.multiple_of(half * c + theirs, 16), quarter)].astype(F32)
                  + rd[i, pl.ds(pl.multiple_of(theirs, 16), quarter)].astype(F32)).astype(BF16)
-        scatter(i).start()
+        for j in range(CUTS):
+            scatter(i, j).start()
         d2d(i).wait_send()
 
     def column(ref, at, size, lane):
@@ -122,51 +127,72 @@
         picked = jnp.where(lax.broadcasted_iota(jnp.int32, block.shape, 1) == lane, block, 0.0)
         return jnp.sum(picked, axis=1, keepdims=True)
 
-    def out_piece(own_row, i, at_x):
+    def out_piece(own_row, i, j, at_x):
         image = (y if own_row else 1 - y) * images + i
-        return out_hbm.at[image, pl.ds(quarter * at_x, quarter)]
-
-    def final_piece(i):
-        return xg.at[i, pl.ds(half * c + quarter * x, quarter)]
-
-    def exit_copy(kind, i):
-        sems = (ex_s.at[kind, i], ex_r.at[kind, i])
+        return out_hbm.at[image, pl.ds(quarter * at_x + cut * j, cut)]
+
+    def final_piece(i, j):
+        return xg.at[i, pl.ds(half * c + quarter * x + cut * j, cut)]
+
+    def exit_copy(kind, i, j):
+        sems = (ex_s.at[kind, i, j], ex_r.at[kind, i, j])
         if kind == 0:
-            return send(final_piece(i), out_piece(True, i, x), *sems, row)
+            return send(final_piece(i, j), out_piece(True, i, j, x), *sems, row)
         if kind in (1, 2):
-            return send(final_piece(i), out_piece(True, i, x), *sems, across if kind == 1 else sib)
+            return send(final_piece(i, j), out_piece(True, i, j, x), *sems, across if kind == 1 else sib)
         if kind in (3, 4):
-            ref = out_piece(False, i, x)
+            ref = out_piece(False, i, j, x)
             return send(ref, ref, *sems, across if kind == 3 else sib)
-        ref = out_piece(kind == 5, i, 1 - x)
+        ref = out_piece(kind == 5, i, j, 1 - x)
         return send(ref, ref, *sems, sib)
 
-    def exit_local(i):
-        return pltpu.make_async_copy(final_piece(i), out_piece(True, i, x), x_sem.at[i])
+    def exit_local(i, j):
+        return pltpu.make_async_copy(final_piece(i, j), out_piece(True, i, j, x), lo_sem.at[i, j])
 
     def stage_c(k):
         i, s = k % images, k // images
-        scatter(i).wait_recv()
-        at = pl.multiple_of(half * c + quarter * x, 16)
-        bias = column(vt, at, quarter, 8 + s)
-        new = xg[i, pl.ds(at, quarter)].astype(F32) + (acc[i] + rr[i].astype(F32))[:, :tokens] + bias
-        xg[i, pl.ds(at, quarter)] = new.astype(BF16)
-        scatter(i).wait_send()
+        for j in range(CUTS):
+            scatter(i, j).wait_recv()
+            at = pl.multiple_of(half * c + quarter * x + cut * j, 16)
+            bias = column(vt, at, cut, 8 + s)
+            got = acc[i, cut * j:cut * (j + 1)] + rr[i, cut * j:cut * (j + 1)].astype(F32)
+            new = xg[i, pl.ds(at, cut)].astype(F32) + got[:, :tokens] + bias
+            xg[i, pl.ds(at, cut)] = new.astype(BF16)
+
+            @pl.when((s == 3) & (c == y))
+            def _():
+                exit_copy(1, i, j).start()
+                exit_copy(2, i, j).start()
+                exit_local(i, j).start()
+
+            @pl.when((s == 3) & (c != y))
+            def _():
+                exit_copy(0, i, j).start()
+
+        for j in range(CUTS):
+            scatter(i, j).wait_send()
 
         @pl.when(s < 3)
         def _():
             gather(0, i).start()
             gather(1, i).start()
 
-        @pl.when((s == 3) & (c == y))
-        def _():
-            exit_copy(1, i).start()
-            exit_copy(2, i).start()
-            exit_local(i).start()
-
-        @pl.when((s == 3) & (c != y))
-        def _():
-            exit_copy(0, i).start()
+    def exit_row(i):
+        @pl.when(c == y)
+        def _():
+            for j in range(CUTS):
+                send(final_piece(i, j), out_piece(False, i, j, x), ex_s.at[0, i, j], ex_r.at[0, i, j], row).wait_recv()
+                exit_copy(3, i, j).start()
+                exit_copy(4, i, j).start()
+
+    def exit_across(i):
+        @pl.when(c == y)
+        def _():
+            for own_row, kind in ((True, 1), (False, 3)):
+                for j in range(CUTS):
+                    piece = out_piece(own_row, i, j, 1 - x)
+                    send(piece, piece, ex_s.at[kind, i, j], ex_r.at[kind, i, j], across).wait_recv()
+                    exit_copy(5 if own_row else 6, i, j).start()
 
     def stage_d(k):
         i, s = k % images, k // images
@@ -176,16 +202,10 @@
             gather(0, i).wait_recv()
             gather(2, i).start()
 
-        @pl.when((s == 3) & (c == y))
-        def _():
-            send(final_piece(i), out_piece(False, i, x), ex_s.at[0, i], ex_r.at[0, i], row).wait_recv()
-            exit_copy(3, i).start()
-            exit_copy(4, i).start()
-            send(final_piece(i), out_piece(True, i, 1 - x), ex_s.at[1, i], ex_r.at[1, i], across).wait_recv()
-            exit_copy(5, i).start()
-            piece = out_piece(False, i, 1 - x)
-            send(piece, piece, ex_s.at[3, i], ex_r.at[3, i], across).wait_recv()
-            exit_copy(6, i).start()
+        @pl.when(s == 3)
+        def _():
+            exit_row(i)
+            exit_across(i)
 
     def gather_done(k):
         i = k % images
@@ -374,25 +394,29 @@
         lax.fori_loop(0, images, mlp_step, 0)
         return 0
     lax.fori_loop(0, 2, layer, 0)
-    last = 4 * images - 1
-    stage_c(last)
-    stage_d(last - 1)
-    stage_d(last)
+    last = images - 1
+    exit_row(last - 1)
+    stage_c(4 * images - 1)
+    exit_across(last - 1)
+    exit_row(last)
+    exit_across(last)
 
     @pl.when(c == y)
     def _():
         for i in range(images):
-            exit_local(i).wait()
-            for kind in (1, 2, 3, 4, 5, 6):
-                exit_copy(kind, i).wait_send()
+            for j in range(CUTS):
+                exit_local(i, j).wait()
+                for kind in (1, 2, 3, 4, 5, 6):
+                    exit_copy(kind, i, j).wait_send()
 
     @pl.when(c != y)
     def _():
         for i in range(images):
-            exit_copy(0, i).wait_send()
-            for kind, own_row, at_x in ((2, True, x), (4, False, x), (5, True, 1 - x), (6, False, 1 - x)):
-                piece = out_piece(own_row, i, at_x)
-                send(piece, piece, ex_s.at[kind, i], ex_r.at[kind, i], sib).wait_recv()
+            for j in range(CUTS):
+                exit_copy(0, i, j).wait_send()
+                for kind, own_row, at_x in ((2, True, x), (4, False, x), (5, True, 1 - x), (6, False, 1 - x)):
+                    piece = out_piece(own_row, i, j, at_x)
+                    send(piece, piece, ex_s.at[kind, i, j], ex_r.at[kind, i, j], sib).wait_recv()
     for l in range(2):
         for n in range(6):
             w_remote(l, n).wait_send()
@@ -436,8 +460,8 @@
                 vmem((width, 128), F32), vmem((128, 128), F32), vmem((long, 128), F32),
                 dma((2, 6)), dma((2, 6)), dma((2, 6)), dma((9,)), dma((6,)), dma((6,)), dma((images,)),
                 dma((4, images)), dma((4, images)), dma((images,)), dma((images,)),
-                dma((images,)), dma((images,)), dma((3, images)), dma((3, images)),
-                dma((7, images)), dma((7, images)),
+                dma((images, CUTS)), dma((images, CUTS)), dma((3, images)), dma((3, images)),
+                dma((7, images, CUTS)), dma((7, images, CUTS)), dma((images, CUTS)),
             ],
             compiler_params=pltpu.CompilerParams(collective_id=0, has_side_effects=True, vmem_limit_bytes=66_000_000),
             name="encoder",

time: 314 us -> 311 us (level)
  no operation moved by 1% of the time
where the time goes in v5:
time: 311 us
  Pallas kernels  306 us (98%)
  local copies, waits for them, and re-layouts  5.23 us (2%)
    pallas_call x1, Pallas kernels, local_fn(): pl.pallas_call(kernel, out_shape=jax.ShapeDtypeStruct((total, half, token...  306 us

profile of v5, /device:TPU:0, one launch (start us, length us, event | category | flops | bytes accessed | tf_op | source)
XLA Modules:
  0.0 311.3 jit_solution(9384328284295227930)
XLA Ops:
  0.0 306.0 %encoder.1 = bf16[6,576,729]{2,1,0:T(8,128)(2,1)} custom-call(bf16[6,576,729]{2,1,0:T(8,128)(2,1)} %bitcast.14, f32[2,576]{1,0:T(2,128)} %g1_hbm.1, f32[2,576]{1,0:T(2,128)} %g2_hbm.1, f32[2,576]{1,0:T(2,128)} %s1_hbm.1, f32[2,576]{1,0:T(2,128)} %s2_hbm.1, f32[2,576]{1,0:T(2,128)} %bo_hbm.1, f32[2,576]{1,0:T(2,128)} %bd_hbm.1, f32[2,4,72]{2,1,0:T(4,128)} %bq_hbm.1, ...), custom_call_target="tpu_custom_call" | custom-call | tf_op jit(solution)/shard_map/encoder/pallas_call | solution.py:445
  306.1 5.2 %copy.18 = bf16[6,729,576]{1,2,0:T(8,128)(2,1)} copy(bf16[6,729,576]{1,2,0:T(8,128)(2,1)} %bitcast.13) | data formatting | bytes 10077696

commit v6 on v5

--- a/solution.py
+++ b/solution.py
@@ -24,8 +24,9 @@
 
 
 def kernel(x_hbm, g1_hbm, g2_hbm, s1_hbm, s2_hbm, bo_hbm, bd_hbm, bq_hbm, bv_hbm, bup_hbm, wq_hbm, wk_hbm, wv_hbm, wo_hbm, wup_hbm, wdn_hbm, out_hbm,
-           xg, h, part, rd, rs, rr, acc, q3, k3, v3, att, hid, wqkv, wo, wup, wdn, vraw, craw, uraw, vpad, cpad, upad, vt, ct, ut,
-           loc_sem, ws_sem, wr_sem, vec_sem, vec_s, vec_r, x_sem, en_s, en_r, d2_s, d2_r, rs_s, rs_r, ag_s, ag_r, ex_s, ex_r, lo_sem):
+           xg, h, part, rd, rs, rr, acc, q3, k3, v3, att, every, hid, wqkv, wo, wup, wdn, vraw, craw, uraw, vpad, cpad, upad, vt, ct, ut,
+           loc_sem, ws_sem, wr_sem, vec_sem, vec_s, vec_r, x_sem, en_s, en_r, d2_s, d2_r, rs_s, rs_r, ag_s, ag_r, ex_s, ex_r, lo_sem,
+           at_s, at_r, hx_s, hx_r, wo_loc, wo_s, wo_r):
     dp, y, ty = lax.axis_index("dp"), lax.axis_index("tx"), lax.axis_index("ty")
     c, x = ty % 2, ty // 2
     images, width, tokens = xg.shape
@@ -39,7 +40,7 @@
     row = (dp, 1 - y, ty)
 
     barrier = pltpu.get_barrier_semaphore()
-    for peer in (sib, across, row):
+    for peer in (sib, across, row, (dp, y, 3 - ty), (dp, 1 - y, ty + 1 - 2 * c)):
         pl.semaphore_signal(barrier, inc=1, device_id=peer, device_id_type=MESH)
 
     def send(src, dst, ssem, rsem, peer):
@@ -50,7 +51,6 @@
         res = []
         for t, w in enumerate((wq_hbm, wk_hbm, wv_hbm)):
             res.append((w.at[l], wqkv.at[l, y, pl.ds(rows_q * t, rows_q)]))
-        res.append((wo_hbm.at[l], wo.at[l, y]))
         res.append((wup_hbm.at[l], wup.at[l, pl.ds(half * y, half)]))
         res.append((wdn_hbm.at[l], wdn.at[l, pl.ds(half * y, half)]))
         return res
@@ -67,6 +67,55 @@
         for n in ns:
             w_local(l, n).wait()
             w_remote(l, n).wait_recv()
+
+    def wo_send(l, kind):
+        peer = ((dp, y, 2 * x + y), (dp, y, 2 * (1 - x) + y), (dp, 1 - y, 2 * x + y))[kind]
+        return send(wo_hbm.at[l], wo.at[l, ty], wo_s.at[l, kind], wo_r.at[l, ty], peer)
+
+    def wo_local(l):
+        return pltpu.make_async_copy(wo_hbm.at[l], wo.at[l, ty], wo_loc.at[l])
+
+    def wo_here(l):
+        @pl.when(c == y)
+        def _():
+            wo_local(l).start()
+
+        @pl.when(c != y)
+        def _():
+            wo_send(l, 0).start()
+
+    def wo_pass(l, n):
+        ref = wo.at[l, 2 * x + n]
+        return send(ref, ref, wo_s.at[l, 3 + n], wo_r.at[l, 2 * x + n], across)
+
+    def wo_came(l, block):
+        send(wo_hbm.at[l], wo.at[l, block], wo_s.at[l, 0], wo_r.at[l, block], across).wait_recv()
+
+    def wo_fwd(l):
+        @pl.when(c != y)
+        def _():
+            for n in range(2):
+                wo_came(l, 2 * x + n)
+                wo_pass(l, n).start()
+
+    def wo_wait(l):
+        for n in range(2):
+            wo_came(l, 2 * (1 - x) + n)
+
+        @pl.when(c == y)
+        def _():
+            wo_local(l).wait()
+            wo_came(l, ty + 1 - 2 * c)
+
+    def wo_end(l):
+        for kind in (1, 2):
+            wo_send(l, kind).wait_send()
+
+        @pl.when(c != y)
+        def _():
+            wo_send(l, 0).wait_send()
+            for n in range(2):
+                wo_pass(l, n).wait_send()
 
     def mine_in(i):
         return pltpu.make_async_copy(x_hbm.at[y * images + i], xg.at[i, pl.ds(half * y, half)], x_sem.at[i])
@@ -267,19 +316,45 @@
             return 0
         lax.fori_loop(0, heads, one_head, 0, unroll=2)
 
+        packed = jnp.concatenate([att[n] for n in range(heads)], axis=0).astype(BF16)
+        every[i, pl.ds(pl.multiple_of(rows_q * ty, 16), rows_q), :] = packed
+        att_copy(0, i).start()
+        att_copy(1, i).start()
+
+    def att_copy(kind, i):
+        owner = ty if kind < 2 else (ty + 2) % 4
+        ref = every.at[i, pl.ds(rows_q * owner, rows_q)]
+        return send(ref, ref, at_s.at[kind, i], at_r.at[kind, i], across if kind == 0 else sib)
+
+    def half_copy(i):
+        ref = xg.at[i, pl.ds(half * c, half)]
+        return send(ref, ref, hx_s.at[i], hx_r.at[i], sib)
+
+    def att_fwd(i):
+        att_copy(0, i).wait_recv()
+        att_copy(2, i).start()
+
+    def att_out(l, i):
         @pl.when(i == 0)
         def _():
+            wo_wait(l)
+        att_copy(1, i).wait_recv()
+        att_copy(2, i).wait_recv()
+        at = pl.multiple_of(half * c, 16)
+        value = tn_dot(wo[l].reshape(width, half), every[i]) + column(vt, at, half, 8 + 2 * l)
+        xg[i, pl.ds(at, half)] = (xg[i, pl.ds(at, half)].astype(F32) + value[:, :tokens]).astype(BF16)
+        half_copy(i).start()
+        for kind in range(3):
+            att_copy(kind, i).wait_send()
+
+    def mlp(l, i):
+        half_copy(i).wait_recv()
+        half_copy(i).wait_send()
+        norm(i, 2 * l + 1)
+
+        @pl.when(i == 0)
+        def _():
             w_wait(l, (3,))
-        packed = jnp.concatenate([att[n] for n in range(heads)], axis=0).astype(BF16)
-        hid[0:rows_q, :] = packed
-        project(l, i, lambda hf: tn_dot(wo[l, hf], hid[0:rows_q, :]))
-
-    def mlp(l, i):
-        norm(i, 2 * l + 1)
-
-        @pl.when(i == 0)
-        def _():
-            w_wait(l, (4,))
         units = wup.shape[2]
         for a in range(0, units, 384):
             b = min(units, a + 384)
@@ -288,12 +363,14 @@
 
         @pl.when(i == 0)
         def _():
-            w_wait(l, (5,))
+            att_fwd(images - 1)
+            att_out(l, images - 1)
+            w_wait(l, (4,))
         project(l, i, lambda hf: nn_dot(wdn[l, pl.ds(pl.multiple_of(half * hf, 16), half)], hid[...]))
 
     for i in range(images):
         mine_in(i).start()
-    for n in range(6):
+    for n in range(5):
         w_local(0, n).start()
     vecs = (g1_hbm, g2_hbm, s1_hbm, s2_hbm, bo_hbm, bd_hbm)
     small = [pltpu.make_async_copy(v, vraw.at[y, n], vec_sem.at[n]) for n, v in enumerate(vecs)]
@@ -302,17 +379,22 @@
     for copy in small:
         copy.start()
     vec_row = [send(v, vraw.at[y, n], vec_s.at[n], vec_r.at[n], row) for n, v in enumerate(vecs)]
-    pl.semaphore_wait(barrier, 3)
+    pl.semaphore_wait(barrier, 5)
     entry_row(0).start()
     for copy in vec_row:
         copy.start()
-    for n in range(4):
+    wo_here(0)
+    wo_send(0, 1).start()
+    for n in range(3):
         w_remote(0, n).start()
+    wo_send(0, 2).start()
     for i in range(1, images):
         entry_row(i).start()
-    for n in range(4, 6):
+    for n in range(3, 5):
         w_remote(0, n).start()
-    for n in range(6):
+    wo_here(1)
+    wo_send(1, 1).start()
+    for n in range(5):
         w_local(1, n).start()
 
     layers = wup.shape[0]
@@ -352,42 +434,49 @@
             def _():
                 gather_done(k)
             attend(l, i)
-            stage_b(k)
+
+            @pl.when(i >= 1)
+            def _():
+                att_fwd(i - 1)
+
+            @pl.when((l > 0) & (i == 0))
+            def _():
+                stage_c(k - 1)
+
+            @pl.when((l > 0) & (i <= 1))
+            def _():
+                stage_d(k - 2)
+
+            @pl.when(i == 0)
+            def _():
+                wo_fwd(l)
 
             @pl.when(k == 0)
             def _():
                 for j in range(1, images):
                     entry(j)
-                for n in range(6):
+                for n in range(3):
                     w_remote(1, n).start()
-
-            @pl.when(k >= 1)
-            def _():
-                stage_c(k - 1)
-
-            @pl.when(k >= 2)
-            def _():
-                stage_d(k - 2)
+                wo_send(1, 2).start()
+                for n in range(3, 5):
+                    w_remote(1, n).start()
+
+            @pl.when(i >= 1)
+            def _():
+                att_out(l, i - 1)
             return 0
         lax.fori_loop(0, images, attn_step, 0)
 
         def mlp_step(i, _):
             k = 2 * images * l + images + i
-            early = k == images
-
-            @pl.when(early)
-            def _():
-                stage_c(k - 1)
-                stage_d(k - 2)
-            gather_done(k)
             mlp(l, i)
             stage_b(k)
 
-            @pl.when(jnp.logical_not(early))
+            @pl.when(i >= 1)
             def _():
                 stage_c(k - 1)
 
-            @pl.when(jnp.logical_not(early))
+            @pl.when(i >= 2)
             def _():
                 stage_d(k - 2)
             return 0
@@ -418,7 +507,8 @@
                     piece = out_piece(own_row, i, j, at_x)
                     send(piece, piece, ex_s.at[kind, i, j], ex_r.at[kind, i, j], sib).wait_recv()
     for l in range(2):
-        for n in range(6):
+        wo_end(l)
+        for n in range(5):
             w_remote(l, n).wait_send()
 
 
@@ -452,16 +542,17 @@
                 vmem((images, half, cols), BF16), vmem((images, half // 2, cols), BF16),
                 vmem((images, half // 2, cols), BF16), vmem((images, half // 2, cols), F32),
                 vmem((heads, 128, cols), BF16), vmem((heads, 128, cols), BF16), vmem((heads, head, cols), BF16),
-                vmem((heads, head, cols), F32), vmem((units, cols), BF16),
-                vmem((layers, 2, 3 * rows_q, half), BF16), vmem((layers, 2, rows_q, half), BF16),
+                vmem((heads, head, cols), F32), vmem((images, width, cols), BF16), vmem((units, cols), BF16),
+                vmem((layers, 2, 3 * rows_q, half), BF16), vmem((layers, 4, rows_q, half), BF16),
                 vmem((layers, width, units), BF16), vmem((layers, width, units), BF16),
                 vmem((2, 6, layers, half), F32), vmem((2, layers, heads, head), F32), vmem((layers, units), F32),
                 vmem((2, 128, lanes), F32), vmem((128, 128), F32), vmem((128, long), F32),
                 vmem((width, 128), F32), vmem((128, 128), F32), vmem((long, 128), F32),
-                dma((2, 6)), dma((2, 6)), dma((2, 6)), dma((9,)), dma((6,)), dma((6,)), dma((images,)),
+                dma((2, 5)), dma((2, 5)), dma((2, 5)), dma((9,)), dma((6,)), dma((6,)), dma((images,)),
                 dma((4, images)), dma((4, images)), dma((images,)), dma((images,)),
                 dma((images, CUTS)), dma((images, CUTS)), dma((3, images)), dma((3, images)),
                 dma((7, images, CUTS)), dma((7, images, CUTS)), dma((images, CUTS)),
+                dma((3, images)), dma((3, images)), dma((images,)), dma((images,)), dma((2,)), dma((2, 5)), dma((2, 4)),
             ],
             compiler_params=pltpu.CompilerParams(collective_id=0, has_side_effects=True, vmem_limit_bytes=66_000_000),
             name="encoder",

time: 311 us -> 288 us (0.926)
  Pallas kernels: 306 us -> 283 us
    pallas_call x1, Pallas kernels: 306 us -> 283 us  [local_fn(): pl.pallas_call(kernel, out_shape=jax.ShapeDtypeStruct((total, half, token...]
where the time goes in v6:
time: 288 us
  Pallas kernels  283 us (98%)
  local copies, waits for them, and re-layouts  5.23 us (2%)
    pallas_call x1, Pallas kernels, local_fn(): pl.pallas_call(kernel, out_shape=jax.ShapeDtypeStruct((total, half, token...  283 us

profile of v6, /device:TPU:0, one launch (start us, length us, event | category | flops | bytes accessed | tf_op | source)
XLA Modules:
  0.0 288.1 jit_solution(11187991920788552814)
XLA Ops:
  0.0 282.8 %encoder.1 = bf16[6,576,729]{2,1,0:T(8,128)(2,1)} custom-call(bf16[6,576,729]{2,1,0:T(8,128)(2,1)} %bitcast.14, f32[2,576]{1,0:T(2,128)} %g1_hbm.1, f32[2,576]{1,0:T(2,128)} %g2_hbm.1, f32[2,576]{1,0:T(2,128)} %s1_hbm.1, f32[2,576]{1,0:T(2,128)} %s2_hbm.1, f32[2,576]{1,0:T(2,128)} %bo_hbm.1, f32[2,576]{1,0:T(2,128)} %bd_hbm.1, f32[2,4,72]{2,1,0:T(4,128)} %bq_hbm.1, ...), custom_call_target="tpu_custom_call" | custom-call | tf_op jit(solution)/shard_map/encoder/pallas_call | solution.py:535
  282.8 5.2 %copy.18 = bf16[6,729,576]{1,2,0:T(8,128)(2,1)} copy(bf16[6,729,576]{1,2,0:T(8,128)(2,1)} %bitcast.13) | data formatting | bytes 10077696

commit v7 on v6

--- a/solution.py
+++ b/solution.py
@@ -24,7 +24,7 @@
 
 
 def kernel(x_hbm, g1_hbm, g2_hbm, s1_hbm, s2_hbm, bo_hbm, bd_hbm, bq_hbm, bv_hbm, bup_hbm, wq_hbm, wk_hbm, wv_hbm, wo_hbm, wup_hbm, wdn_hbm, out_hbm,
-           xg, h, part, rd, rs, rr, acc, q3, k3, v3, att, every, hid, wqkv, wo, wup, wdn, vraw, craw, uraw, vpad, cpad, upad, vt, ct, ut,
+           xg, h, part, rd, rs, rr, acc, q3, k3, v3, att, every, wqkv, wo, wup, wdn, vraw, craw, uraw, vpad, cpad, upad, vt, ct, ut,
            loc_sem, ws_sem, wr_sem, vec_sem, vec_s, vec_r, x_sem, en_s, en_r, d2_s, d2_r, rs_s, rs_r, ag_s, ag_r, ex_s, ex_r, lo_sem,
            at_s, at_r, hx_s, hx_r, wo_loc, wo_s, wo_r):
     dp, y, ty = lax.axis_index("dp"), lax.axis_index("tx"), lax.axis_index("ty")
@@ -35,6 +35,7 @@
     rows_q = 3 * wq_hbm.shape[1] // 3
     head = v3.shape[1]
     heads = v3.shape[0]
+    units = wup.shape[2]
     sib = (dp, y, ty + 1 - 2 * c)
     across = (dp, y, (ty + 2) % 4)
     row = (dp, 1 - y, ty)
@@ -159,17 +160,16 @@
         ref = xg.at[i, pl.ds(half * c + quarter * src_x, quarter)]
         return send(ref, ref, ag_s.at[kind, i], ag_r.at[kind, i], across if kind == 0 else sib)
 
-    def stage_b(k):
+    def stage_b(k, slot):
         i = k % images
         d2d(i).wait_recv()
         mine, theirs = quarter * x, quarter * (1 - x)
-        acc[i] = (part[pl.ds(pl.multiple_of(half * c + mine, 16), quarter)].astype(F32)
+        acc[i] = (part[pl.ds(pl.multiple_of(half * slot + mine, 16), quarter)].astype(F32)
                   + rd[i, pl.ds(pl.multiple_of(mine, 16), quarter)].astype(F32))
-        rs[i] = (part[pl.ds(pl.multiple_of(half * c + theirs, 16), quarter)].astype(F32)
+        rs[i] = (part[pl.ds(pl.multiple_of(half * slot + theirs, 16), quarter)].astype(F32)
                  + rd[i, pl.ds(pl.multiple_of(theirs, 16), quarter)].astype(F32)).astype(BF16)
         for j in range(CUTS):
             scatter(i, j).start()
-        d2d(i).wait_send()
 
     def column(ref, at, size, lane):
         block = ref[pl.ds(at, size), :]
@@ -234,27 +234,20 @@
                 exit_copy(3, i, j).start()
                 exit_copy(4, i, j).start()
 
-    def exit_across(i):
+    def exit_across(i, own_row):
+        kind = 1 if own_row else 3
+
         @pl.when(c == y)
         def _():
-            for own_row, kind in ((True, 1), (False, 3)):
-                for j in range(CUTS):
-                    piece = out_piece(own_row, i, j, 1 - x)
-                    send(piece, piece, ex_s.at[kind, i, j], ex_r.at[kind, i, j], across).wait_recv()
-                    exit_copy(5 if own_row else 6, i, j).start()
+            for j in range(CUTS):
+                piece = out_piece(own_row, i, j, 1 - x)
+                send(piece, piece, ex_s.at[kind, i, j], ex_r.at[kind, i, j], across).wait_recv()
+                exit_copy(5 if own_row else 6, i, j).start()
 
     def stage_d(k):
-        i, s = k % images, k // images
-
-        @pl.when(s < 3)
-        def _():
-            gather(0, i).wait_recv()
-            gather(2, i).start()
-
-        @pl.when(s == 3)
-        def _():
-            exit_row(i)
-            exit_across(i)
+        i = k % images
+        gather(0, i).wait_recv()
+        gather(2, i).start()
 
     def gather_done(k):
         i = k % images
@@ -276,25 +269,14 @@
             gain, shift = column(vt, n * quarter, quarter, s), column(vt, n * quarter, quarter, 4 + s)
             h[b, 0:tokens] = ((xg[i, b].astype(F32) - mean) * inv * gain + shift).astype(BF16)
 
-    def project(l, i, make):
-        def body(n, _):
-            hf = (1 - c) * (1 - n) + c * n
-            part[pl.ds(pl.multiple_of(half * hf, 16), half)] = make(hf).astype(BF16)
-
-            @pl.when(n == 0)
-            def _():
-                d2d(i).start()
-            return 0
-        lax.fori_loop(0, 2, body, 0)
-
     factor = (head ** -0.5) * 1.4426950408889634
 
     def attend(l, i):
+        @pl.when(i == 0)
+        def _():
+            w_wait(l, (0, 1, 2))
         norm(i, 2 * l)
         for t, ref in enumerate((q3, k3, v3)):
-            @pl.when(i == 0)
-            def _():
-                w_wait(l, (t,))
             at = pl.ds(rows_q * t, rows_q)
             value = nn_dot(wqkv[l, 0, at], h[:half]) + nn_dot(wqkv[l, 1, at], h[half:])
             for n in range(heads):
@@ -314,7 +296,7 @@
             p = (e * (1.0 / jnp.sum(e, axis=0, keepdims=True))).astype(BF16)
             att[n] = nn_dot(v3[n, :, :edge], p)
             return 0
-        lax.fori_loop(0, heads, one_head, 0, unroll=2)
+        lax.fori_loop(0, heads, one_head, 0, unroll=4)
 
         packed = jnp.concatenate([att[n] for n in range(heads)], axis=0).astype(BF16)
         every[i, pl.ds(pl.multiple_of(rows_q * ty, 16), rows_q), :] = packed
@@ -335,8 +317,7 @@
         att_copy(2, i).start()
 
     def att_out(l, i):
-        @pl.when(i == 0)
-        def _():
+        if isinstance(i, int) and i == 0:
             wo_wait(l)
         att_copy(1, i).wait_recv()
         att_copy(2, i).wait_recv()
@@ -347,26 +328,111 @@
         for kind in range(3):
             att_copy(kind, i).wait_send()
 
-    def mlp(l, i):
+    def down(l, i, hf, slot):
+        at = pl.multiple_of(half * hf, 16)
+        part[pl.ds(pl.multiple_of(half * slot, 16), half)] = nn_dot(wdn[l, pl.ds(at, half)], every[i, 0:units]).astype(BF16)
+
+    def mlp_first(l, i):
+        k = 2 * images * l + images + i
         half_copy(i).wait_recv()
         half_copy(i).wait_send()
+        @pl.when(i == 0)
+        def _():
+            w_wait(l, (3,))
         norm(i, 2 * l + 1)
-
-        @pl.when(i == 0)
-        def _():
-            w_wait(l, (3,))
-        units = wup.shape[2]
-        for a in range(0, units, 384):
-            b = min(units, a + 384)
+        for a in range(0, units, 640):
+            b = min(units, a + 640)
             u = tn_dot(wup[l, :, a:b], h[...]) + column(ut, a, b - a, l)
-            hid[a:b, :] = gelu(u).astype(BF16)
+            every[i, a:b, :] = gelu(u).astype(BF16)
 
         @pl.when(i == 0)
         def _():
             att_fwd(images - 1)
             att_out(l, images - 1)
-            w_wait(l, (4,))
-        project(l, i, lambda hf: nn_dot(wdn[l, pl.ds(pl.multiple_of(half * hf, 16), half)], hid[...]))
+            w_local(l, 4).wait()
+
+        @pl.when((c == y) & (i >= 1))
+        def _():
+            stage_b(k - 1, c)
+
+        @pl.when((c == y) & (i >= 2))
+        def _():
+            stage_c(k - 2)
+
+        @pl.when((c != y) & (i >= 1))
+        def _():
+            d2d(i - 1).wait_send()
+        down(l, i, y, y)
+
+        @pl.when(c != y)
+        def _():
+            d2d(i).start()
+
+    def mlp_second(l, i):
+        k = 2 * images * l + images + i
+
+        @pl.when(i == 0)
+        def _():
+            @pl.when(c == y)
+            def _():
+                stage_b(k + images - 1, c)
+                stage_c(k + images - 2)
+
+            @pl.when(c != y)
+            def _():
+                d2d(images - 1).wait_send()
+            w_remote(l, 4).wait_recv()
+
+        @pl.when((c == y) & (i >= 1))
+        def _():
+            d2d(i - 1).wait_send()
+        down(l, i, 1 - y, (1 - y + i * (c + y - 2 * c * y)) % 2)
+
+        @pl.when(c == y)
+        def _():
+            d2d(i).start()
+
+            @pl.when(i == 1)
+            def _():
+                stage_c(k + images - 2)
+
+            @pl.when(i >= 1)
+            def _():
+                send_on(l, k - 1)
+
+        @pl.when((c != y) & (i >= 1))
+        def _():
+            stage_b(k - 1, (c + i - 1) % 2)
+
+        @pl.when((c != y) & (i >= 2))
+        def _():
+            stage_c(k - 2)
+
+    def send_on(l, k):
+        @pl.when(l == 0)
+        def _():
+            stage_d(k)
+
+        @pl.when(l == 1)
+        def _():
+            exit_across(k % images, True)
+
+    def mlp_end(l):
+        k = 2 * images * l + 2 * images - 1
+
+        @pl.when(c == y)
+        def _():
+            d2d(images - 1).wait_send()
+            send_on(l, k)
+
+        @pl.when(c != y)
+        def _():
+            stage_b(k, (c + images - 1) % 2)
+            stage_c(k - 1)
+
+            @pl.when(l == 0)
+            def _():
+                stage_d(k - 2)
 
     for i in range(images):
         mine_in(i).start()
@@ -439,11 +505,11 @@
             def _():
                 att_fwd(i - 1)
 
-            @pl.when((l > 0) & (i == 0))
+            @pl.when((l > 0) & (i == 0) & (c != y))
             def _():
                 stage_c(k - 1)
 
-            @pl.when((l > 0) & (i <= 1))
+            @pl.when((l > 0) & (i <= 1) & (c != y))
             def _():
                 stage_d(k - 2)
 
@@ -461,34 +527,35 @@
                 for n in range(3, 5):
                     w_remote(1, n).start()
 
-            @pl.when(i >= 1)
-            def _():
-                att_out(l, i - 1)
+            @pl.when(i == images - 1)
+            def _():
+                for j in range(images - 1):
+                    att_out(l, j)
             return 0
         lax.fori_loop(0, images, attn_step, 0)
 
-        def mlp_step(i, _):
-            k = 2 * images * l + images + i
-            mlp(l, i)
-            stage_b(k)
-
-            @pl.when(i >= 1)
-            def _():
-                stage_c(k - 1)
-
-            @pl.when(i >= 2)
-            def _():
-                stage_d(k - 2)
+        def first_step(i, _):
+            mlp_first(l, i)
             return 0
-        lax.fori_loop(0, images, mlp_step, 0)
+        lax.fori_loop(0, images, first_step, 0)
+
+        def second_step(i, _):
+            mlp_second(l, i)
+            return 0
+        lax.fori_loop(0, images, second_step, 0)
+
+        mlp_end(l)
         return 0
     lax.fori_loop(0, 2, layer, 0)
-    last = images - 1
-    exit_row(last - 1)
-    stage_c(4 * images - 1)
-    exit_across(last - 1)
-    exit_row(last)
-    exit_across(last)
+
+    @pl.when(c != y)
+    def _():
+        stage_c(4 * images - 1)
+    for i in range(images):
+        exit_row(i)
+        if i >= 1:
+            exit_across(i - 1, False)
+    exit_across(images - 1, False)
 
     @pl.when(c == y)
     def _():
@@ -542,7 +609,7 @@
                 vmem((images, half, cols), BF16), vmem((images, half // 2, cols), BF16),
                 vmem((images, half // 2, cols), BF16), vmem((images, half // 2, cols), F32),
                 vmem((heads, 128, cols), BF16), vmem((heads, 128, cols), BF16), vmem((heads, head, cols), BF16),
-                vmem((heads, head, cols), F32), vmem((images, width, cols), BF16), vmem((units, cols), BF16),
+                vmem((heads, head, cols), F32), vmem((images, width, cols), BF16),
                 vmem((layers, 2, 3 * rows_q, half), BF16), vmem((layers, 4, rows_q, half), BF16),
                 vmem((layers, width, units), BF16), vmem((layers, width, units), BF16),
                 vmem((2, 6, layers, half), F32), vmem((2, layers, heads, head), F32), vmem((layers, units), F32),

time: 288 us -> 285 us (0.990)
  Pallas kernels: 283 us -> 280 us
    pallas_call x1, Pallas kernels: 283 us -> 280 us  [local_fn(): pl.pallas_call(kernel, out_shape=jax.ShapeDtypeStruct((total, half, token...]
where the time goes in v7:
time: 285 us
  Pallas kernels  280 us (98%)
  local copies, waits for them, and re-layouts  5.23 us (2%)
    pallas_call x1, Pallas kernels, local_fn(): pl.pallas_call(kernel, out_shape=jax.ShapeDtypeStruct((total, half, token...  280 us

profile of v7, /device:TPU:0, one launch (start us, length us, event | category | flops | bytes accessed | tf_op | source)
XLA Modules:
  0.0 285.0 jit_solution(8586915160313234684)
XLA Ops:
  0.0 279.8 %encoder.1 = bf16[6,576,729]{2,1,0:T(8,128)(2,1)} custom-call(bf16[6,576,729]{2,1,0:T(8,128)(2,1)} %bitcast.14, f32[2,576]{1,0:T(2,128)} %g1_hbm.1, f32[2,576]{1,0:T(2,128)} %g2_hbm.1, f32[2,576]{1,0:T(2,128)} %s1_hbm.1, f32[2,576]{1,0:T(2,128)} %s2_hbm.1, f32[2,576]{1,0:T(2,128)} %bo_hbm.1, f32[2,576]{1,0:T(2,128)} %bd_hbm.1, f32[2,4,72]{2,1,0:T(4,128)} %bq_hbm.1, ...), custom_call_target="tpu_custom_call" | custom-call | tf_op jit(solution)/shard_map/encoder/pallas_call | solution.py:602
  279.8 5.2 %copy.18 = bf16[6,729,576]{1,2,0:T(8,128)(2,1)} copy(bf16[6,729,576]{1,2,0:T(8,128)(2,1)} %bitcast.13) | data formatting | bytes 10077696

commit v8 on v7

--- a/solution.py
+++ b/solution.py
@@ -164,12 +164,13 @@
         i = k % images
         d2d(i).wait_recv()
         mine, theirs = quarter * x, quarter * (1 - x)
+        for j in range(CUTS):
+            rows = pl.ds(cut * j, cut)
+            rs[i, rows] = (part[pl.ds(pl.multiple_of(half * slot + theirs + cut * j, 16), cut)].astype(F32)
+                           + rd[i, pl.ds(pl.multiple_of(theirs + cut * j, 16), cut)].astype(F32)).astype(BF16)
+            scatter(i, j).start()
         acc[i] = (part[pl.ds(pl.multiple_of(half * slot + mine, 16), quarter)].astype(F32)
                   + rd[i, pl.ds(pl.multiple_of(mine, 16), quarter)].astype(F32))
-        rs[i] = (part[pl.ds(pl.multiple_of(half * slot + theirs, 16), quarter)].astype(F32)
-                 + rd[i, pl.ds(pl.multiple_of(theirs, 16), quarter)].astype(F32)).astype(BF16)
-        for j in range(CUTS):
-            scatter(i, j).start()
 
     def column(ref, at, size, lane):
         block = ref[pl.ds(at, size), :]

time: 285 us -> 285 us (level)
  no operation moved by 1% of the time
where the time goes in v8:
time: 285 us
  Pallas kernels  279 us (98%)
  local copies, waits for them, and re-layouts  5.23 us (2%)
    pallas_call x1, Pallas kernels, local_fn(): pl.pallas_call(kernel, out_shape=jax.ShapeDtypeStruct((total, half, token...  279 us

profile of v8, /device:TPU:0, one launch (start us, length us, event | category | flops | bytes accessed | tf_op | source)
XLA Modules:
  0.0 284.7 jit_solution(6347893028441790864)
XLA Ops:
  0.0 279.5 %encoder.1 = bf16[6,576,729]{2,1,0:T(8,128)(2,1)} custom-call(bf16[6,576,729]{2,1,0:T(8,128)(2,1)} %bitcast.14, f32[2,576]{1,0:T(2,128)} %g1_hbm.1, f32[2,576]{1,0:T(2,128)} %g2_hbm.1, f32[2,576]{1,0:T(2,128)} %s1_hbm.1, f32[2,576]{1,0:T(2,128)} %s2_hbm.1, f32[2,576]{1,0:T(2,128)} %bo_hbm.1, f32[2,576]{1,0:T(2,128)} %bd_hbm.1, f32[2,4,72]{2,1,0:T(4,128)} %bq_hbm.1, ...), custom_call_target="tpu_custom_call" | custom-call | tf_op jit(solution)/shard_map/encoder/pallas_call | solution.py:603
  279.5 5.2 %copy.18 = bf16[6,729,576]{1,2,0:T(8,128)(2,1)} copy(bf16[6,729,576]{1,2,0:T(8,128)(2,1)} %bitcast.13) | data formatting | bytes 10077696
